TPU v7x, 256 devices: a whole 4x4x8 slice. The times are simulated.
256 devices in a mesh: dp: 64 (over x_lo, y, z), mp: 2 (over core), fsdp: 2 (over x_hi).
Axes of the slice: x: 4 (x_hi: 2, x_lo: 2; x = x_hi * 2 + x_lo), y: 4, z: 8, core: 2. Of those that a mesh axis runs over, the one named last changes fastest.
Arguments:
- features: bfloat16 [5, 1024, 4096], P(None, ('dp', 'fsdp')), may hold values from -24 to 24
- memory_bank: bfloat16 [4096, 32, 1024], P(('dp', 'fsdp')), may hold values from -1 to 1
- memory_fill: int32 [4096], P(('dp', 'fsdp')), may hold values from 0 to 32
- left_keys: bfloat16 [4096, 64, 1024], P(('dp', 'fsdp'), None, 'mp'), may hold values from -400 to 400
- left_values: bfloat16 [4096, 64, 1024], P(('dp', 'fsdp'), None, 'mp'), may hold values from -6 to 6
- left_length: int32 [4096], P(('dp', 'fsdp')), may hold values from 0 to 64
- w_query: bfloat16 [1024, 1024], P('fsdp', 'mp'), may hold values from -0.1875 to 0.1875
- w_key: bfloat16 [1024, 1024], P('fsdp', 'mp'), may hold values from -0.1875 to 0.1875
- w_value: bfloat16 [1024, 1024], P('fsdp', 'mp'), may hold values from -0.1875 to 0.1875
- w_out: bfloat16 [1024, 1024], P('mp', 'fsdp'), may hold values from -0.1875 to 0.1875
- w_up: bfloat16 [1024, 4096], P('fsdp', 'mp'), may hold values from -0.1875 to 0.1875
- w_down: bfloat16 [4096, 1024], P('mp', 'fsdp'), may hold values from -0.09375 to 0.09375
- out_gain: float32 [1024], replicated, may hold values from 0.1 to 1.9
Outputs:
- layer_out: bfloat16 [4096, 5, 1024], P(('dp', 'fsdp'))
- memory_next: bfloat16 [4096, 1024], P(('dp', 'fsdp'))
- center_keys: bfloat16 [4096, 4, 1024], P(('dp', 'fsdp'), None, 'mp')
- center_values: bfloat16 [4096, 4, 1024], P(('dp', 'fsdp'), None, 'mp')
All inputs are finite; a program needn't handle non-finite values.
Results may differ from a plain program's by a relative error of at most 0.0095.
Values may be sent and summed in bfloat16 or wider, within the bound.
A program may use at most 128 MiB of HBM per device.

v0:
```python
import jax
import jax.numpy as jnp
from jax import lax
from jax.sharding import PartitionSpec as P

HD = 64
GROUP = 4


epsilon = 1e-05
masked_score = -1e30


def side_by_side(arrays, axis, dim, along):
    ends, at = ([], 0)
    for a in arrays[:-1]:
        at += a.shape[along]
        ends.append(at)
    both = jnp.concatenate(arrays, axis=along)
    return tuple(jnp.split(lax.all_gather(both, axis, axis=dim, tiled=True), ends, axis=along))


def in_order(tiles, dim):
    dims = list(tiles.shape[1:])
    dims[dim] *= tiles.shape[0]
    return jnp.moveaxis(tiles, 0, dim).reshape(dims)


def copy_for_each(array, axis):
    count = lax.axis_size(axis)
    return lax.all_to_all(
        jnp.broadcast_to(array[None], (count, *array.shape)), axis, 0, 0, tiled=True
    )


def collect(array, axis, dim):
    return in_order(copy_for_each(array, axis), dim)


def taken_together(array, axis):
    everything = copy_for_each(array, axis)
    return jnp.sum(everything.astype(jnp.float32), axis=0)


def normalize(values):
    values = values.astype(jnp.float32)
    average = jnp.mean(values, axis=-1, keepdims=True)
    centred = values - average
    variance = jnp.mean(centred * centred, axis=-1, keepdims=True)
    return centred * lax.rsqrt(variance + epsilon)


def matmul(left, right):
    return jnp.dot(left, right, preferred_element_type=jnp.float32)


def shards(
    features,
    memory_bank,
    memory_fill,
    left_keys,
    left_values,
    left_length,
    w_query,
    w_key,
    w_value,
    w_out,
    w_up,
    w_down,
    out_gain,
):
    frames, width_dev, all_streams = features.shape
    streams, mem_slots, width = memory_bank.shape
    left_slots = left_keys.shape[1]
    head_cols = w_query.shape[1]
    head_count = head_cols // HD
    flattened = features.reshape(frames * width_dev, all_streams)
    n_dp = lax.axis_size("dp")
    n_fsdp = lax.axis_size("fsdp")
    arrived = lax.all_to_all(flattened, ("dp", "fsdp"), split_axis=1, concat_axis=0, tiled=True)
    arrived = arrived.reshape(n_dp * n_fsdp, frames, width_dev, streams)
    inputs = jnp.transpose(arrived, (3, 1, 0, 2)).reshape(streams, frames, width)
    normed = normalize(inputs).astype(jnp.bfloat16)
    summary = jnp.mean(normed[:, :GROUP, :].astype(jnp.float32), axis=1).astype(jnp.bfloat16)
    query_rows = jnp.concatenate([normed, summary[:, None, :]], axis=1).reshape(-1, width)
    key_rows = jnp.concatenate([normed.reshape(-1, width), memory_bank.reshape(-1, width)], axis=0)
    pieces = side_by_side((w_query, w_key, w_value), "fsdp", 0, 1)
    query_sums = matmul(query_rows, pieces[0])
    key_sums = matmul(key_rows, pieces[1])
    value_sums = matmul(key_rows, pieces[2])
    query_proj = query_sums.astype(jnp.bfloat16)
    key_proj = key_sums.astype(jnp.bfloat16)
    value_proj = value_sums.astype(jnp.bfloat16)
    group_total = streams * frames
    query_h = query_proj.reshape(streams, frames + 1, head_count, HD)
    ckey_h = key_proj[:group_total].reshape(streams, frames, head_count, HD)
    cval_h = value_proj[:group_total].reshape(streams, frames, head_count, HD)
    mkey_h = key_proj[group_total:].reshape(streams, mem_slots, head_count, HD)
    mval_h = value_proj[group_total:].reshape(streams, mem_slots, head_count, HD)
    lkey_h = left_keys.reshape(streams, left_slots, head_count, HD)
    lval_h = left_values.reshape(streams, left_slots, head_count, HD)
    not_summary = jnp.arange(frames + 1, dtype=jnp.int32) < frames
    mem_ok = jnp.arange(mem_slots, dtype=jnp.int32)[None, :] >= (mem_slots - memory_fill)[:, None]
    mem_mask = mem_ok[:, None, None, :] & not_summary[None, None, :, None]
    left_ok = (
        jnp.arange(left_slots, dtype=jnp.int32)[None, :] >= (left_slots - left_length)[:, None]
    )
    left_mask = left_ok[:, None, None, :]
    scale = HD ** (-0.5)
    score_mem = (
        jnp.einsum("sqhd,skhd->shqk", query_h, mkey_h, preferred_element_type=jnp.float32) * scale
    )
    score_left = (
        jnp.einsum("sqhd,skhd->shqk", query_h, lkey_h, preferred_element_type=jnp.float32) * scale
    )
    score_group = (
        jnp.einsum("sqhd,skhd->shqk", query_h, ckey_h, preferred_element_type=jnp.float32) * scale
    )
    score_mem = jnp.where(mem_mask, score_mem, masked_score)
    score_left = jnp.where(left_mask, score_left, masked_score)
    top = jnp.maximum(
        jnp.maximum(
            jnp.max(score_mem, axis=-1, keepdims=True), jnp.max(score_left, axis=-1, keepdims=True)
        ),
        jnp.max(score_group, axis=-1, keepdims=True),
    )
    exp_mem = jnp.exp(score_mem - top)
    exp_left = jnp.exp(score_left - top)
    exp_group = jnp.exp(score_group - top)
    totals = (
        jnp.sum(exp_mem, axis=-1, keepdims=True)
        + jnp.sum(exp_left, axis=-1, keepdims=True)
        + jnp.sum(exp_group, axis=-1, keepdims=True)
    )
    prob_mem = (exp_mem / totals).astype(jnp.bfloat16)
    prob_left = (exp_left / totals).astype(jnp.bfloat16)
    prob_group = (exp_group / totals).astype(jnp.bfloat16)
    attended = jnp.einsum("shqk,skhd->sqhd", prob_mem, mval_h, preferred_element_type=jnp.float32)
    attended = attended + jnp.einsum(
        "shqk,skhd->sqhd", prob_left, lval_h, preferred_element_type=jnp.float32
    )
    attended = attended + jnp.einsum(
        "shqk,skhd->sqhd", prob_group, cval_h, preferred_element_type=jnp.float32
    )
    attended = attended.astype(jnp.bfloat16).reshape(streams * (frames + 1), head_cols)
    attn_part = matmul(attended, collect(w_out, "fsdp", 1))
    attn_out = (
        taken_together(attn_part.astype(jnp.bfloat16), "mp")
        .astype(jnp.float32)
        .reshape(streams, frames + 1, width)
    )
    memory_next = jnp.tanh(attn_out[:, frames, :]).astype(jnp.bfloat16)
    hidden_state = inputs.astype(jnp.float32) + attn_out[:, :frames, :]
    h_norm = normalize(hidden_state).astype(jnp.bfloat16).reshape(-1, width)
    up_sums = matmul(h_norm, lax.all_gather(w_up, "fsdp", axis=0, tiled=True))
    hidden = jax.nn.gelu(up_sums, approximate=True).astype(jnp.bfloat16)
    down_part = matmul(hidden, collect(w_down, "fsdp", 1))
    down_proj = taken_together(down_part.astype(jnp.bfloat16), "mp").astype(jnp.float32)
    layer_out = (
        (normalize(hidden_state.reshape(-1, width) + down_proj) * out_gain)
        .astype(jnp.bfloat16)
        .reshape(streams, frames, width)
    )
    center_keys = key_proj[:group_total].reshape(streams, frames, head_cols)[:, :GROUP, :]
    center_values = value_proj[:group_total].reshape(streams, frames, head_cols)[:, :GROUP, :]
    return (layer_out, memory_next, center_keys, center_values)


def solution(mesh):
    in_specs = (
        P(None, ("dp", "fsdp"), None),
        P(("dp", "fsdp"), None, None),
        P(("dp", "fsdp")),
        P(("dp", "fsdp"), None, "mp"),
        P(("dp", "fsdp"), None, "mp"),
        P(("dp", "fsdp")),
        P("fsdp", "mp"),
        P("fsdp", "mp"),
        P("fsdp", "mp"),
        P("mp", "fsdp"),
        P("fsdp", "mp"),
        P("mp", "fsdp"),
        P(),
    )
    out_specs = (
        P(("dp", "fsdp"), None, None),
        P(("dp", "fsdp"), None),
        P(("dp", "fsdp"), None, "mp"),
        P(("dp", "fsdp"), None, "mp"),
    )
    return jax.shard_map(shards, mesh=mesh, in_specs=in_specs, out_specs=out_specs, check_vma=False)
```

profile of v0, /device:TPU:169, one launch (start us, length us, event | category | flops | bytes accessed | tf_op | source)
XLA Modules:
  0.0 225.4 jit_solution(4706145072289891522)
XLA Ops:
  7.2 2.6 %pad_maximum_fusion.1 = bf16[512,1536]{1,0:T(8,128)(2,1)} fusion(bf16[512,512]{1,0:T(8,128)(2,1)} %param.21, bf16[512,512]{1,0:T(8,128)(2,1)} %param.20, bf16[512,512]{1,0:T(8,128)(2,1)} %param.19), kind=kLoop, calls=%fused_computation.21 | loop fusion | flops 4718592 | bytes 3145728 | tf_op jit(solution)/shard_map/concatenate | solution.py:19
  9.9 1.0 all_to_all.22
  10.9 1.5 copy.134
  12.4 2.4 %reshape.262 = bf16[128,2,640]{2,1,0:T(2,128)(2,1)} reshape(bf16[128,32,40]{2,1,0:T(8,128)(2,1)S(1)} %bitcast.55) | data formatting | bytes 655360
  14.8 12.7 %all-to-all-start = ((bf16[128,2,640]{2,1,0:T(2,128)(2,1)}), bf16[128,2,640]{2,1,0:T(2,128)(2,1)S(1)}, u32[]{:S(2)}, u32[]{:S(2)}) async-start(bf16[128,2,640]{2,1,0:T(2,128)(2,1)} %reshape.262), calls=%async_computation | async-start | bytes 655360 | tf_op jit(solution)/shard_map/all_to_all | solution.py:80
  27.5 0.7 all-gather.5.cloned.1.call-update
  28.4 3.6 %reshape.246 = bf16[32,64,8,64]{3,2,1,0:T(8,128)(2,1)} reshape(bf16[32,64,512]{2,1,0:T(8,128)(2,1)S(1)} %copy-done.8) | data formatting | bytes 4194304 | tf_op jit(solution)/shard_map/reshape | solution.py:100
  32.0 6.3 %reshape.248 = bf16[32,64,8,64]{3,2,1,0:T(8,128)(2,1)} reshape(bf16[32,64,512]{2,1,0:T(8,128)(2,1)} %param.17) | data formatting | bytes 4194304 | tf_op jit(solution)/shard_map/reshape | solution.py:101
  38.6 2.5 %copy.155 = bf16[2048,512]{0,1:T(8,128)(2,1)} copy(bf16[2048,512]{1,0:T(8,128)(2,1)S(1)} %copy-done.10) | data formatting | bytes 4194304 | tf_op args[11]
  41.1 0.7 broadcast_and_fusion
  41.8 1.1 broadcast_in_dim.36
  42.9 4.6 %all-to-all-start.1 = ((bf16[2,512,512]{1,2,0:T(8,128)(2,1)}), bf16[2,512,512]{1,2,0:T(8,128)(2,1)}, u32[]{:S(2)}, u32[]{:S(2)}) async-start(bf16[2,512,512]{1,2,0:T(8,128)(2,1)} %broadcast_in_dim.36), calls=%async_computation.1 | async-start | bytes 2097152 | tf_op jit(solution)/shard_map/all_to_all | solution.py:31
  47.5 1.6 reshape.263
  49.1 1.4 copy.135
  50.5 5.4 %copy.137 = f32[32,5,128,8]{3,2,1,0:T(8,128)} copy(f32[32,5,128,8]{2,0,3,1:T(8,128)S(1)} %bitcast.50) | data formatting | bytes 1310720 | tf_op jit(solution)/shard_map/convert_element_type | solution.py:153
  56.4 1.4 copy.136
  57.8 10.1 %reshape.258 = f32[160,1024]{1,0:T(8,128)} reshape(f32[32,5,128,8]{3,2,1,0:T(8,128)} %copy.137) | data formatting | bytes 1310720 | tf_op jit(solution)/shard_map/convert_element_type | solution.py:153
  69.1 1.1 copy.140
  70.2 0.9 reshape.243
  71.5 3.4 %convolution_convert_fusion = bf16[1184,512]{1,0:T(8,128)(2,1)S(1)} fusion(bf16[1024,1024]{1,0:T(8,128)(2,1)} %bitcast.58, bf16[160,1024]{1,0:T(8,128)(2,1)S(1)} %multiply_convert_fusion.2, bf16[1024,1536]{1,0:T(8,128)(2,1)} %all-gather.3.cloned.1.call-done), kind=kOutput, calls=%fused_computation.4 | convolution fusion | flops 1246969856 | bytes 4685824 | tf_op jit(solution)/shard_map/dot_general | solution.py:54
  75.0 3.1 %convolution_convert_fusion.1 = bf16[1184,512]{1,0:T(8,128)(2,1)S(1)} fusion(bf16[1024,1024]{1,0:T(8,128)(2,1)S(1)} %bitcast.59, bf16[160,1024]{1,0:T(8,128)(2,1)S(1)} %multiply_convert_fusion.2, bf16[1024,1536]{1,0:T(8,128)(2,1)} %all-gather.3.cloned.1.call-done), kind=kOutput, calls=%fused_computation.5 | convolution fusion | flops 1246969856 | bytes 4685824 | tf_op jit(solution)/shard_map/dot_general | solution.py:54
  78.2 1.0 slice.38
  79.2 0.9 reshape.247
  80.2 1.6 convolution_convert_fusion.4
  82.0 0.9 reshape.249
  83.0 1.1 reshape.245
  84.1 3.9 %reshape.242 = bf16[32,32,8,64]{3,2,1,0:T(8,128)(2,1)} reshape(bf16[1024,512]{1,0:T(8,128)(2,1)} %slice.38) | data formatting | bytes 2097152 | tf_op jit(solution)/shard_map/reshape | solution.py:99
  88.0 0.5 fusion.77
  88.6 1.3 fusion.78
  89.9 0.4 copy-done.1
  90.2 2.4 %fusion.79 = (f32[32,8,6]{2,1,0:T(8,128)S(1)}, f32[32,8,6,64]{3,2,1,0:T(8,128)S(1)}) fusion(bf16[32,64,8,64]{3,2,1,0:T(8,128)(2,1)S(1)} %copy-done.1, bf16[32,6,8,64]{3,2,1,0:T(8,128)(2,1)S(1)} %reshape.244, pred[32,64]{1,0:T(8,128)(4,1)S(1)} %iota_compare_fusion), kind=kOutput, calls=%fused_computation.105 | convolution fusion | flops 12876288 | bytes 2695168 | tf_op jit(solution)/shard_map/sqhd,skhd->shqk/dot_general | solution.py:114
  92.6 0.7 fusion.48
  93.3 0.4 fusion.50
  93.7 0.7 fusion.49
  94.5 0.5 convolution_bitcast_fusion
  95.0 1.2 copy-done.9
  96.2 0.9 fusion.10
  97.1 1.5 copy-done.5
  98.6 1.5 fusion.42
  100.4 1.9 convolution_convert_fusion.2
  102.4 39.4 %all_to_all.33 = bf16[2,192,1024]{2,1,0:T(8,128)(2,1)S(1)} all-to-all(bf16[2,192,1024]{2,1,0:T(8,128)(2,1)S(1)} %broadcast_in_dim.37), channel_id=1, replica_groups=mesh['dp'=64,'mp'=2,'fsdp'=2] {'mp'}, dimensions={0} | all-to-all | bytes 1572864 | tf_op jit(solution)/shard_map/all_to_all | solution.py:31
  141.8 2.5 %broadcast_in_dim.38 = bf16[2,2048,512]{1,2,0:T(8,128)(2,1)} broadcast(bf16[2048,512]{0,1:T(8,128)(2,1)S(1)} %copy-done.2), dimensions={1,2} | broadcast | bytes 6291456 | tf_op jit(solution)/shard_map/broadcast_in_dim | solution.py:32
  144.3 5.7 %all-to-all-start.3 = ((bf16[2,2048,512]{1,2,0:T(8,128)(2,1)}), bf16[2,2048,512]{1,2,0:T(8,128)(2,1)}, u32[]{:S(2)}, u32[]{:S(2)}) async-start(bf16[2,2048,512]{1,2,0:T(8,128)(2,1)} %broadcast_in_dim.38), calls=%async_computation.3 | async-start | bytes 8388608 | tf_op jit(solution)/shard_map/all_to_all | solution.py:31
  150.2 0.8 reshape.256
  151.2 1.0 copy-done.3
  152.2 2.0 copy.160
  154.2 2.8 %fusion.76 = (f32[32,5]{0,1:T(8,128)S(1)}, f32[32,5,1024]{0,2,1:T(8,128)S(1)}) fusion(f32[32,5,1024]{0,2,1:T(8,128)} %copy.160, f32[32,5,128,8]{0,3,2,1:T(8,128)} %copy-done), kind=kLoop, calls=%fused_computation.102 | loop fusion | flops 327520 | bytes 1966720 | tf_op jit(solution)/shard_map/reduce_sum | solution.py:47
  157.0 0.3 multiply_reduce_fusion.1
  157.4 1.4 multiply_convert_fusion.1
  158.9 2.0 copy.154
  160.9 0.9 reshape.253
  161.8 1.4 fusion.68
  163.1 0.7 copy.210
  163.8 0.7 slice.45
  164.5 1.7 slice.46
  166.1 32.6 %all-to-all-done.3 = bf16[2,2048,512]{1,2,0:T(8,128)(2,1)} async-done(((bf16[2,2048,512]{1,2,0:T(8,128)(2,1)}), bf16[2,2048,512]{1,2,0:T(8,128)(2,1)}, u32[]{:S(2)}, u32[]{:S(2)}) %all-to-all-start.3) | async-done | bytes 4194336 | tf_op jit(solution)/shard_map/all_to_all | solution.py:31
  198.7 6.1 %convolution_convert_fusion.3 = bf16[160,1024]{1,0:T(8,128)(2,1)S(1)} fusion(bf16[2048,1024]{0,1:T(8,128)(2,1)} %bitcast.14, bf16[160,1024]{1,0:T(8,128)(2,1)} %reshape.253, bf16[1024,2048]{1,0:T(8,128)(2,1)} %all-gather.5.cloned.1.call-done), kind=kOutput, calls=%fused_computation.45 | convolution fusion | flops 1345290240 | bytes 9043968 | tf_op jit(solution)/shard_map/dot_general | solution.py:54
  204.9 5.1 %all_to_all.34 = bf16[2,160,1024]{2,1,0:T(8,128)(2,1)S(1)} all-to-all(bf16[2,160,1024]{2,1,0:T(8,128)(2,1)S(1)} %broadcast_in_dim.39), channel_id=1, replica_groups=mesh['dp'=64,'mp'=2,'fsdp'=2] {'mp'}, dimensions={0} | all-to-all | bytes 1310720 | tf_op jit(solution)/shard_map/all_to_all | solution.py:31
  210.1 1.1 reduce_sum.120
  211.2 3.0 %copy.156 = f32[32,5,1024]{0,2,1:T(8,128)} copy(f32[32,5,1024]{2,1,0:T(8,128)} %reduce_sum.120) | data formatting | bytes 1310720 | tf_op jit(solution)/shard_map/reduce_sum | solution.py:42
  214.2 2.0 fusion.75
  216.2 0.4 multiply_reduce_fusion
  216.9 0.4 multiply_convert_fusion
  217.3 1.2 copy.157
  (90 shorter events, 4.2 us)
Async XLA Ops:
  7.2 2.7 %copy-start.18 = (bf16[5,8,4096]{2,1,0:T(8,128)(2,1)S(1)}, bf16[5,8,4096]{2,1,0:T(8,128)(2,1)}, u32[]{:S(2)}) copy-start(bf16[5,8,4096]{2,1,0:T(8,128)(2,1)} %param.13) | copy-start | bytes 983044
  7.2 64.4 %all-gather.3.cloned.1.call-start = ((), (), s32[]{:S(2)}) async-start(), calls=%async_computation.5 | async-start | bytes 4718592 | tf_op jit(solution)/shard_map/all_gather | solution.py:20
  12.4 15.9 %copy-start.22 = (s32[32]{0:T(128)S(1)}, s32[32]{0:T(128)}, u32[]{:S(2)}) copy-start(s32[32]{0:T(128)} %param.15) | copy-start | bytes 388
  14.8 13.6 %copy-start.8 = (bf16[32,64,512]{2,1,0:T(8,128)(2,1)S(1)}, bf16[32,64,512]{2,1,0:T(8,128)(2,1)}, u32[]{:S(2)}) copy-start(bf16[32,64,512]{2,1,0:T(8,128)(2,1)} %param.16) | copy-start | bytes 6291460
  14.8 27.0 %all-to-all-start = ((bf16[128,2,640]{2,1,0:T(2,128)(2,1)}), bf16[128,2,640]{2,1,0:T(2,128)(2,1)S(1)}, u32[]{:S(2)}, u32[]{:S(2)}) async-start(bf16[128,2,640]{2,1,0:T(2,128)(2,1)} %reshape.262), calls=%async_computation | async-start | bytes 655360 | tf_op jit(solution)/shard_map/all_to_all | solution.py:80
  27.5 171.2 %all-gather.5.cloned.1.call-start = ((), (), s32[]{:S(2)}) async-start(), calls=%async_computation.6 | async-start | bytes 6291456 | tf_op jit(solution)/shard_map/all_gather | solution.py:155
  32.0 6.3 %copy-start.15 = (bf16[512,512]{1,0:T(8,128)(2,1)S(1)}, bf16[512,512]{1,0:T(8,128)(2,1)}, u32[]{:S(2)}) copy-start(bf16[512,512]{1,0:T(8,128)(2,1)} %param.22) | copy-start | bytes 1572868
  32.0 6.6 %copy-start.10 = (bf16[2048,512]{1,0:T(8,128)(2,1)S(1)}, bf16[2048,512]{1,0:T(8,128)(2,1)}, u32[]{:S(2)}) copy-start(bf16[2048,512]{1,0:T(8,128)(2,1)} %param.24) | copy-start | bytes 6291460
  38.3 2.7 %copy-start.23 = (s32[32]{0:T(128)S(1)}, s32[32]{0:T(128)}, u32[]{:S(2)}) copy-start(s32[32]{0:T(128)} %param.18) | copy-start | bytes 388
  42.9 57.5 %all-to-all-start.1 = ((bf16[2,512,512]{1,2,0:T(8,128)(2,1)}), bf16[2,512,512]{1,2,0:T(8,128)(2,1)}, u32[]{:S(2)}, u32[]{:S(2)}) async-start(bf16[2,512,512]{1,2,0:T(8,128)(2,1)} %broadcast_in_dim.36), calls=%async_computation.1 | async-start | bytes 2097152 | tf_op jit(solution)/shard_map/all_to_all | solution.py:31
  57.8 10.4 %copy-start = (f32[32,5,128,8]{0,3,2,1:T(8,128)}, f32[32,5,128,8]{0,3,2,1:T(8,128)S(1)}, u32[]{:S(2)}) copy-start(f32[32,5,128,8]{0,3,2,1:T(8,128)S(1)} %copy.136) | copy-start | bytes 1966084
  68.8 2.3 %copy-start.6 = (f32[160,1024]{1,0:T(8,128)S(1)}, f32[160,1024]{1,0:T(8,128)}, u32[]{:S(2)}) copy-start(f32[160,1024]{1,0:T(8,128)} %reshape.258) | copy-start | bytes 1966084
  71.5 3.5 %copy-start.21 = (bf16[32,32,1024]{2,1,0:T(8,128)(2,1)S(1)}, bf16[32,32,1024]{2,1,0:T(8,128)(2,1)}, u32[]{:S(2)}) copy-start(bf16[32,32,1024]{2,1,0:T(8,128)(2,1)} %param.14) | copy-start | bytes 6291460
  75.0 3.2 %copy-start.4 = (bf16[1184,512]{1,0:T(8,128)(2,1)}, bf16[1184,512]{1,0:T(8,128)(2,1)S(1)}, u32[]{:S(2)}) copy-start(bf16[1184,512]{1,0:T(8,128)(2,1)S(1)} %convolution_convert_fusion) | copy-start | bytes 3637252
  75.0 4.2 %copy-start.11 = (bf16[160,512]{1,0:T(8,128)(2,1)}, bf16[160,512]{1,0:T(8,128)(2,1)S(1)}, u32[]{:S(2)}) copy-start(bf16[160,512]{1,0:T(8,128)(2,1)S(1)} %slice.41) | copy-start | bytes 491524
  78.2 2.0 copy-start.16
  78.2 3.8 %copy-start.13 = (bf16[160,512]{1,0:T(8,128)(2,1)}, bf16[160,512]{1,0:T(8,128)(2,1)S(1)}, u32[]{:S(2)}) copy-start(bf16[160,512]{1,0:T(8,128)(2,1)S(1)} %slice.42) | copy-start | bytes 491524
  78.2 4.8 %slice-start = ((bf16[1184,512]{1,0:T(8,128)(2,1)}), bf16[1024,512]{1,0:T(8,128)(2,1)S(1)}, s32[]{:S(2)}) async-start(bf16[1184,512]{1,0:T(8,128)(2,1)} %copy-done.4), calls=%async_computation.7 | async-start | bytes 2097152 | tf_op jit(solution)/shard_map/slice | solution.py:98
  84.1 4.0 %copy-start.7 = (bf16[32,5,8,64]{3,2,1,0:T(8,128)(2,1)S(1)}, bf16[32,5,8,64]{3,2,1,0:T(8,128)(2,1)}, u32[]{:S(2)}) copy-start(bf16[32,5,8,64]{3,2,1,0:T(8,128)(2,1)} %reshape.247) | copy-start | bytes 491524
  84.1 4.5 %copy-start.19 = (pred[32,6,32]{2,1,0:T(8,128)(4,1)S(1)}, pred[32,6,32]{2,1,0:T(8,128)(4,1)}, u32[]{:S(2)}) copy-start(pred[32,6,32]{2,1,0:T(8,128)(4,1)} %broadcast_and_fusion) | copy-start | bytes 18436
  88.0 2.2 copy-start.1
  92.6 1.9 copy-start.17
  94.4 1.8 copy-start.9
  96.2 2.4 %copy-start.5 = (bf16[32,64,8,64]{3,2,1,0:T(8,128)(2,1)S(1)}, bf16[32,64,8,64]{3,2,1,0:T(8,128)(2,1)}, u32[]{:S(2)}) copy-start(bf16[32,64,8,64]{3,2,1,0:T(8,128)(2,1)} %reshape.248) | copy-start | bytes 6291460
  100.1 41.7 %copy-start.2 = (bf16[2048,512]{0,1:T(8,128)(2,1)S(1)}, bf16[2048,512]{0,1:T(8,128)(2,1)}, u32[]{:S(2)}) copy-start(bf16[2048,512]{0,1:T(8,128)(2,1)} %copy.155) | copy-start | bytes 6291460
  144.3 5.8 %copy-start.12 = (bf16[160,512]{1,0:T(8,128)(2,1)S(1)}, bf16[160,512]{1,0:T(8,128)(2,1)}, u32[]{:S(2)}) copy-start(bf16[160,512]{1,0:T(8,128)(2,1)} %copy-done.11) | copy-start | bytes 491524
  144.3 5.8 %copy-start.14 = (bf16[160,512]{1,0:T(8,128)(2,1)S(1)}, bf16[160,512]{1,0:T(8,128)(2,1)}, u32[]{:S(2)}) copy-start(bf16[160,512]{1,0:T(8,128)(2,1)} %copy-done.13) | copy-start | bytes 491524
  144.3 54.4 %all-to-all-start.3 = ((bf16[2,2048,512]{1,2,0:T(8,128)(2,1)}), bf16[2,2048,512]{1,2,0:T(8,128)(2,1)}, u32[]{:S(2)}, u32[]{:S(2)}) async-start(bf16[2,2048,512]{1,2,0:T(8,128)(2,1)} %broadcast_in_dim.38), calls=%async_computation.3 | async-start | bytes 8388608 | tf_op jit(solution)/shard_map/all_to_all | solution.py:31
  151.2 1.0 copy-start.3
  216.2 0.7 copy-start.20
Sparse Core Ops, SparseCore 0:
  10.0 61.5 all-gather.2
  73.3 68.4 all-gather.4
where the time goes:
time: 226 us; the launch traced here: 225 us
  local copies, waits for them, and re-layouts  70.6 us (31%)
  blocking collectives  44.5 us (20%)
  waiting for transfers between devices  33.6 us (15%)
  matrix products  23.2 us (10%)
  starting transfers between devices  23.1 us (10%)
  other arithmetic  15.7 us (7%)
  between operations  14.7 us (7%)
    all_to_all x2, blocking collectives, copy_for_each(): lax.all_to_all(jnp.broadcast_to(array[None], (count, *array.shape)), axis...  44.5 us
    all_to_all x2, waiting for transfers between devices, copy_for_each(): lax.all_to_all(jnp.broadcast_to(array[None], (count, *array.shape)), axis...  32.6 us
    convert_element_type x3, local copies, waits for them, and re-layouts, shards(): hidden_state = inputs.astype(jnp.float32) + attn_out[:, :frames, :]  16.9 us
    dot_general x5, matrix products, matmul(): return jnp.dot(left, right, preferred_element_type=jnp.float32)  16.1 us
    unnamed x55, local copies, waits for them, and re-layouts  15 us
    all_to_all x1, starting transfers between devices, shards(): lax.all_to_all(flattened, ('dp', 'fsdp'), split_axis=1, concat_axis=0, ti...  12.7 us
    all_to_all x2, starting transfers between devices, copy_for_each(): lax.all_to_all(jnp.broadcast_to(array[None], (count, *array.shape)), axis...  10.3 us
    reshape x1, local copies, waits for them, and re-layouts, shards(): lval_h = left_values.reshape(streams, left_slots, head_count, HD)  6.34 us
  transfers between devices with their start and end apart: 5, of which 2 were waited for; matrix products, arithmetic and copies ran while one was open for 39% of the time, Pallas kernels for 0%

commit v1 on v0

v1 whole, which is shorter than its diff:
```python
import functools

import jax
import jax.numpy as jnp
from jax import lax
from jax.experimental import pallas as pl
from jax.experimental.pallas import tpu as pltpu
from jax.sharding import PartitionSpec as P

HD = 64
GROUP = 4
FRAMES = 5
MEM = 32
LEFT = 64
STR = 32
ROWS = 8
KEYS = 112
UNITS = 12
EPS = 1e-05
MASKED = -1e30
F32 = jnp.float32
BF16 = jnp.bfloat16


def dot(a, b):
    return jnp.dot(a, b, preferred_element_type=F32)


def normalized(x):
    mean = jnp.sum(x, axis=-1, keepdims=True) * (1.0 / x.shape[-1])
    cent = x - mean
    var = jnp.sum(cent * cent, axis=-1, keepdims=True) * (1.0 / x.shape[-1])
    return cent * lax.rsqrt(var + EPS)


def kernel(
    fill,
    length,
    feat_hbm,
    mem_hbm,
    lk_hbm,
    lv_hbm,
    wq_hbm,
    wk_hbm,
    wv_hbm,
    wo_hbm,
    wu_hbm,
    wd_hbm,
    gain,
    out,
    mem_next,
    center_k,
    center_v,
    feat,
    gath,
    blocks,
    held,
    perm,
    rows,
    xp,
    x,
    n,
    own,
    got,
    memory,
    keys,
    values,
    q,
    att,
    part,
    part_in,
    down,
    down_out,
    down_in,
    l_sem,
    g_send,
    g_recv,
    h_send,
    h_recv,
    c_send,
    c_recv,
    f_send,
    f_recv,
    e_send,
    e_recv,
):
    d = lax.axis_index("dp")
    m = lax.axis_index("mp")
    f = lax.axis_index("fsdp")
    xl = lax.div(d, 32)
    y = lax.rem(lax.div(d, 8), 4)
    z = lax.rem(d, 8)
    k = lax.div(d, 2)
    odd = lax.rem(d, 2)
    r = odd * 2 + f
    slot = r * 2 + m
    color = lax.rem(y + 2 * xl, 4)

    def dev(dd, ff, mm):
        return {"dp": dd, "fsdp": ff, "mp": mm}

    def remote(src, dst, send, recv, to):
        return pltpu.make_async_remote_copy(
            src_ref=src,
            dst_ref=dst,
            send_sem=send,
            recv_sem=recv,
            device_id=to,
            device_id_type=pl.DeviceIdType.MESH,
        )

    flipped = d + 32 * (1 - 2 * xl)
    up_d = xl * 32 + lax.rem(y + 1, 4) * 8 + z
    down_d = xl * 32 + lax.rem(y + 3, 4) * 8 + z
    cross_dev = dev(flipped, 1 - f, m)
    ring = (dev(flipped, f, m), dev(up_d, f, m), dev(down_d, f, m))
    sibling = dev(d, f, 1 - m)

    def load(i, src, dst):
        return pltpu.make_async_copy(src, dst, l_sem.at[i])

    units = [wk_hbm, wv_hbm, wq_hbm, wo_hbm]
    for j in range(4):
        units.append(wu_hbm.at[:, pl.ds(512 * j, 512)])
        units.append(wd_hbm.at[pl.ds(512 * j, 512), :])
    loads = [load(u, units[u], own.at[u]) for u in range(UNITS)]
    load_feat = load(UNITS, feat_hbm, feat)
    load_mem = load(UNITS + 1, mem_hbm, memory)
    load_lk = load(UNITS + 2, lk_hbm, keys.at[:, pl.ds(MEM, LEFT), :])
    load_lv = load(UNITS + 3, lv_hbm, values.at[:, pl.ds(MEM, LEFT), :])
    load_feat.start()
    for c in loads[:4]:
        c.start()
    load_mem.start()
    load_lk.start()
    load_lv.start()
    for c in loads[4:]:
        c.start()

    barrier = pltpu.get_barrier_semaphore()

    def greet(to):
        pl.semaphore_signal(
            barrier, inc=1, device_id=to, device_id_type=pl.DeviceIdType.MESH
        )

    def greet_sources(j, _):
        kk = 2 * j + m
        greet(dev(2 * kk + odd, f, 1 - lax.rem(k, 2)))
        return 0

    lax.fori_loop(0, 16, greet_sources, 0)

    def quad(e):
        s = lax.rem(slot + e, 8)
        rr = lax.div(s, 2)
        return rr, dev(2 * k + lax.div(rr, 2), lax.rem(rr, 2), lax.rem(s, 2))

    def greet_quad(e, _):
        greet(quad(e)[1])
        return 0

    lax.fori_loop(1, 8, greet_quad, 0)
    greet(cross_dev)
    for to in ring:
        greet(to)
    greet(sibling)
    pl.semaphore_wait(barrier, 16 + 7 + 1 + 3 + 1)

    def first_copy(j):
        t = 2 * lax.rem(j + lax.div(k, 2), 16) + (1 - m)
        return remote(
            feat.at[:, :, pl.ds(pl.multiple_of(t * 128, 128), 128)],
            gath.at[lax.div(k, 2)],
            g_send.at[j],
            g_recv.at[lax.div(k, 2)],
            dev(2 * t + odd, f, lax.rem(k, 2)),
        )

    def send_first(j, _):
        first_copy(j).start()
        return 0

    load_feat.wait()
    lax.fori_loop(0, 16, send_first, 0)

    def piece(ref, u, c):
        return ref.at[u, pl.ds(pl.multiple_of(c * 128, 128), 128), :]

    other = lax.rem(color + 2, 4)

    def cross_copy(u):
        return remote(
            piece(own, u, other), piece(got, u, other), c_send.at[u], c_recv.at[u], cross_dev
        )

    def forward_copy(u, i):
        return remote(
            piece(got, u, color), piece(got, u, color), f_send.at[u, i], f_recv.at[u, i], ring[i]
        )

    def wait_got(u, c, sem):
        pltpu.make_async_copy(piece(got, u, c), piece(got, u, c), sem).wait()

    def forward(u):
        wait_got(u, color, c_recv.at[u])
        for i in range(3):
            forward_copy(u, i).start()

    def ready(u):
        wait_got(u, lax.rem(color + 2, 4), f_recv.at[u, 0])
        wait_got(u, lax.rem(color + 3, 4), f_recv.at[u, 1])
        wait_got(u, lax.rem(color + 1, 4), f_recv.at[u, 2])

    for u in range(UNITS):
        loads[u].wait()
        cross_copy(u).start()

    def build_perm(s, _):
        at = lax.broadcasted_iota(jnp.int32, (128, 1024), 0)
        col = lax.broadcasted_iota(jnp.int32, (128, 1024), 1)
        want = (at >> 3) * 64 + lax.rem(s, 2) * 32 + lax.div(s, 2) * 8 + (at & 7)
        perm[pl.ds(pl.multiple_of(s * 128, 128), 128), :] = jnp.where(
            col == want, 1.0, 0.0
        ).astype(BF16)
        return 0

    lax.fori_loop(0, 8, build_perm, 0)
    at = lax.broadcasted_iota(jnp.int32, (STR * ROWS, STR * FRAMES), 0)
    col = lax.broadcasted_iota(jnp.int32, (STR * ROWS, STR * FRAMES), 1)
    rows[...] = jnp.where(col == (at & 7) * STR + (at >> 3), 1.0, 0.0).astype(BF16)
    att[...] = jnp.zeros_like(att)

    def wait_first(j, _):
        pltpu.make_async_copy(gath.at[j], gath.at[j], g_recv.at[j]).wait()
        return 0

    lax.fori_loop(0, 16, wait_first, 0)
    for fr in range(FRAMES):
        turned = gath[:, fr].astype(F32).reshape(128, 128).T.astype(BF16)
        blocks[:, fr] = turned.reshape(4, STR, 128)

    def second_copy(e):
        rr, to = quad(e)
        return remote(blocks.at[rr], held.at[slot], h_send.at[e], h_recv.at[slot], to)

    def send_second(e, _):
        second_copy(e).start()
        return 0

    lax.fori_loop(1, 8, send_second, 0)
    held[slot] = blocks[r]

    forward(0)
    forward(1)

    def wait_second(e, _):
        s = lax.rem(slot + e, 8)
        pltpu.make_async_copy(held.at[s], held.at[s], h_recv.at[s]).wait()
        return 0

    lax.fori_loop(1, 8, wait_second, 0)
    for s in range(8):
        xp[:, pl.ds(128 * s, 128)] = held[s].reshape(STR * FRAMES, 128)
    for h in range(2):
        half = pl.ds(512 * h, 512)
        placed = dot(xp[...], perm[:, half]).astype(BF16)
        x[:, half] = dot(rows[...], placed)

    def split_norm(values_f32, chunk):
        at = pl.ds(pl.multiple_of(chunk * 32, 32), 32)
        b = values_f32.astype(BF16)
        n[0, at, :] = b[:, :512]
        n[1, at, :] = b[:, 512:]

    def first_norm(c, _):
        at = pl.ds(pl.multiple_of(c * 32, 32), 32)
        v = normalized(x[at, :]).astype(BF16).astype(F32).reshape(4, ROWS, 1024)
        row = lax.broadcasted_iota(jnp.int32, v.shape, 1)
        summary = jnp.sum(jnp.where(row < GROUP, v, 0.0), axis=1, keepdims=True) * (1.0 / GROUP)
        v = jnp.where(row == FRAMES, summary, v)
        split_norm(v.reshape(32, 1024), c)
        return 0

    lax.fori_loop(0, 8, first_norm, 0)
    forward(2)

    load_mem.wait()
    load_lk.wait()
    load_lv.wait()

    mine = pl.ds(pl.multiple_of(f * 512, 512), 512)
    theirs = pl.ds(pl.multiple_of((1 - f) * 512, 512), 512)

    def project(u, place, center):
        def memory_rows(c, _):
            at = pl.ds(pl.multiple_of(c * 256, 256), 256)
            sums = dot(memory[at, mine], own[u]) + dot(memory[at, theirs], got[u])
            place[pl.ds(c * 8, 8), pl.ds(0, MEM), :] = sums.astype(BF16).reshape(8, MEM, 512)
            return 0

        lax.fori_loop(0, 4, memory_rows, 0)

        def group_rows(c, _):
            at = pl.ds(pl.multiple_of(c * 64, 64), 64)
            sums = dot(n[f, at, :], own[u]) + dot(n[1 - f, at, :], got[u])
            g = sums.reshape(8, ROWS, 512)
            both = jnp.concatenate([g, jnp.zeros_like(g)], axis=1).astype(BF16)
            place[pl.ds(c * 8, 8), pl.ds(MEM + LEFT, 16), :] = both
            center[pl.ds(c * 8, 8), :, :] = g[:, :GROUP, :].astype(BF16)
            return 0

        lax.fori_loop(0, 4, group_rows, 0)

    ready(0)
    project(0, keys, center_k)
    forward(3)
    ready(1)
    project(1, values, center_v)
    ready(2)
    q[...] = (
        (dot(n[f], own[2]) + dot(n[1 - f], got[2])).astype(BF16).astype(F32) * (HD**-0.5)
    ).reshape(STR, ROWS, 512)

    heads = ROWS
    head_mask = jnp.where(
        (lax.broadcasted_iota(jnp.int32, (heads, 512), 1) >> 6)
        == lax.broadcasted_iota(jnp.int32, (heads, 512), 0),
        1.0,
        0.0,
    )
    queries = FRAMES + 1

    def attend(s):
        q8 = q[s]
        spread = jnp.concatenate(
            [jnp.broadcast_to(q8[i : i + 1], (heads, 512)) * head_mask for i in range(queries)],
            axis=0,
        ).astype(BF16)
        scores = lax.dot_general(
            spread, keys[s], (((1,), (1,)), ((), ())), preferred_element_type=F32
        )
        row = lax.broadcasted_iota(jnp.int32, scores.shape, 0)
        col = lax.broadcasted_iota(jnp.int32, scores.shape, 1)
        seen_mem = (col >= MEM - fill[s]) & (col < MEM) & (row < FRAMES * heads)
        seen_left = (col >= MEM + LEFT - length[s]) & (col < MEM + LEFT + FRAMES)
        scores = jnp.where(seen_mem | seen_left, scores, MASKED)
        e = jnp.exp(scores - jnp.max(scores, axis=-1, keepdims=True))
        probs = (e / jnp.sum(e, axis=-1, keepdims=True)).astype(BF16)
        mixed = dot(probs, values[s]).reshape(queries, heads, 512)
        att[s, pl.ds(0, queries), :] = jnp.sum(mixed * head_mask[None], axis=1)

    def attend_block(b, _):
        forward(4 + b)

        def pair(i, _):
            attend(b * 8 + 2 * i)
            attend(b * 8 + 2 * i + 1)
            return 0

        lax.fori_loop(0, 4, pair, 0)
        return 0

    lax.fori_loop(0, 4, attend_block, 0)

    def exchange(src, dst, i):
        return remote(src, dst, e_send.at[i], e_recv.at[i], sibling)

    ready(3)
    a = att[...].reshape(STR * ROWS, 512).astype(BF16)
    part[f] = dot(a, own[3]).astype(BF16)
    part[1 - f] = dot(a, got[3]).astype(BF16)
    first = exchange(part, part_in, 0)
    first.start()
    first.wait()

    def second_norm(c, _):
        at = pl.ds(pl.multiple_of(c * 32, 32), 32)
        summed = [part[h, at, :].astype(F32) + part_in[h, at, :].astype(F32) for h in range(2)]
        v = x[at, :] + jnp.concatenate(summed, axis=1)
        x[at, :] = v
        split_norm(normalized(v), c)
        return 0

    lax.fori_loop(0, 8, second_norm, 0)
    mem_next[...] = jnp.tanh(x[...].reshape(STR, ROWS, 1024)[:, FRAMES, :]).astype(BF16)

    down[...] = jnp.zeros_like(down)

    def hidden_block(j, _):
        @pl.when(j < 2)
        def _():
            forward(8 + 2 * j)
            forward(9 + 2 * j)

        ready(4 + 2 * j)
        sums = dot(n[f], own[4 + 2 * j]) + dot(n[1 - f], got[4 + 2 * j])
        hid = jax.nn.gelu(sums, approximate=True).astype(BF16)
        ready(5 + 2 * j)
        down[f] += dot(hid, own[5 + 2 * j])
        down[1 - f] += dot(hid, got[5 + 2 * j])
        return 0

    lax.fori_loop(0, 4, hidden_block, 0)
    down_out[...] = down[...].astype(BF16)
    last = exchange(down_out, down_in, 1)
    last.start()
    last.wait()

    def third_norm(c, _):
        at = pl.ds(pl.multiple_of(c * 32, 32), 32)
        summed = [down_out[h, at, :].astype(F32) + down_in[h, at, :].astype(F32) for h in range(2)]
        v = x[at, :] + jnp.concatenate(summed, axis=1)
        w = (normalized(v) * gain[...]).reshape(4, ROWS, 1024)
        out[pl.ds(c * 4, 4), :, :] = w[:, :FRAMES, :].astype(BF16)
        return 0

    lax.fori_loop(0, 8, third_norm, 0)

    def drain_first(j, _):
        first_copy(j).wait_send()
        return 0

    lax.fori_loop(0, 16, drain_first, 0)

    def drain_second(e, _):
        second_copy(e).wait_send()
        return 0

    lax.fori_loop(1, 8, drain_second, 0)

    def drain(u, _):
        cross_copy(u).wait_send()
        for i in range(3):
            forward_copy(u, i).wait_send()
        return 0

    lax.fori_loop(0, UNITS, drain, 0)


def shards(
    features,
    memory_bank,
    memory_fill,
    left_keys,
    left_values,
    left_length,
    w_query,
    w_key,
    w_value,
    w_out,
    w_up,
    w_down,
    out_gain,
):
    memory = memory_bank.reshape(STR * MEM, 1024)
    smem = pl.BlockSpec(memory_space=pltpu.SMEM)
    hbm = pl.BlockSpec(memory_space=pl.ANY)
    vmem = pl.BlockSpec(memory_space=pltpu.VMEM)
    dma = pltpu.SemaphoreType.DMA
    return pl.pallas_call(
        kernel,
        name="layer",
        out_shape=(
            jax.ShapeDtypeStruct((STR, FRAMES, 1024), BF16),
            jax.ShapeDtypeStruct((STR, 1024), BF16),
            jax.ShapeDtypeStruct((STR, GROUP, 512), BF16),
            jax.ShapeDtypeStruct((STR, GROUP, 512), BF16),
        ),
        in_specs=[smem] * 2 + [hbm] * 10 + [vmem],
        out_specs=(vmem,) * 4,
        scratch_shapes=[
            pltpu.VMEM((FRAMES, 8, 4096), BF16),
            pltpu.VMEM((16, FRAMES, 8, 128), BF16),
            pltpu.VMEM((4, FRAMES, STR, 128), BF16),
            pltpu.VMEM((8, FRAMES, STR, 128), BF16),
            pltpu.VMEM((1024, 1024), BF16),
            pltpu.VMEM((STR * ROWS, STR * FRAMES), BF16),
            pltpu.VMEM((STR * FRAMES, 1024), BF16),
            pltpu.VMEM((STR * ROWS, 1024), F32),
            pltpu.VMEM((2, STR * ROWS, 512), BF16),
            pltpu.VMEM((UNITS, 512, 512), BF16),
            pltpu.VMEM((UNITS, 512, 512), BF16),
            pltpu.VMEM((STR * MEM, 1024), BF16),
            pltpu.VMEM((STR, KEYS, 512), BF16),
            pltpu.VMEM((STR, KEYS, 512), BF16),
            pltpu.VMEM((STR, ROWS, 512), F32),
            pltpu.VMEM((STR, ROWS, 512), F32),
            pltpu.VMEM((2, STR * ROWS, 512), BF16),
            pltpu.VMEM((2, STR * ROWS, 512), BF16),
            pltpu.VMEM((2, STR * ROWS, 512), F32),
            pltpu.VMEM((2, STR * ROWS, 512), BF16),
            pltpu.VMEM((2, STR * ROWS, 512), BF16),
            dma((UNITS + 4,)),
            dma((16,)),
            dma((16,)),
            dma((8,)),
            dma((8,)),
            dma((UNITS,)),
            dma((UNITS,)),
            dma((UNITS, 3)),
            dma((UNITS, 3)),
            dma((2,)),
            dma((2,)),
        ],
        compiler_params=pltpu.CompilerParams(
            collective_id=0, has_side_effects=True, vmem_limit_bytes=60 * 1024 * 1024
        ),
    )(
        memory_fill,
        left_length,
        features,
        memory,
        left_keys,
        left_values,
        w_query,
        w_key,
        w_value,
        w_out,
        w_up,
        w_down,
        out_gain.reshape(1, 1024),
    )


def solution(mesh):
    in_specs = (
        P(None, ("dp", "fsdp"), None),
        P(("dp", "fsdp"), None, None),
        P(("dp", "fsdp")),
        P(("dp", "fsdp"), None, "mp"),
        P(("dp", "fsdp"), None, "mp"),
        P(("dp", "fsdp")),
        P("fsdp", "mp"),
        P("fsdp", "mp"),
        P("fsdp", "mp"),
        P("mp", "fsdp"),
        P("fsdp", "mp"),
        P("mp", "fsdp"),
        P(),
    )
    out_specs = (
        P(("dp", "fsdp"), None, None),
        P(("dp", "fsdp"), None),
        P(("dp", "fsdp"), None, "mp"),
        P(("dp", "fsdp"), None, "mp"),
    )
    return jax.shard_map(shards, mesh=mesh, in_specs=in_specs, out_specs=out_specs, check_vma=False)
```

time: 226 us -> 80.1 us (0.35)
  the two profiles are of different devices: /device:TPU:169 before, /device:TPU:1 now
where the time goes in v1:
time: 80.1 us; the launch traced here: 79.8 us
  Pallas kernels  72.5 us (91%)
  local copies, waits for them, and re-layouts  6.67 us (8%)
    pallas_call x1, Pallas kernels, shards(): pl.pallas_call(kernel, name='layer', out_shape=(jax.ShapeDtypeStruct((STR...  72.5 us
    unnamed x3, local copies, waits for them, and re-layouts  4.68 us
    pallas_call x1, local copies, waits for them, and re-layouts, shards(): pl.pallas_call(kernel, name='layer', out_shape=(jax.ShapeDtypeStruct((STR...  1.99 us

profile of v1, /device:TPU:1, one launch (start us, length us, event | category | flops | bytes accessed | tf_op | source)
XLA Modules:
  0.0 79.8 jit_solution(3015610135718833046)
XLA Ops:
  0.6 72.5 %layer.1 = (bf16[32,5,1024]{2,1,0:T(8,128)(2,1)}, bf16[32,1024]{1,0:T(8,128)(2,1)}, bf16[32,4,512]{2,1,0:T(4,128)(2,1)}, bf16[32,4,512]{2,1,0:T(4,128)(2,1)}) custom-call(s32[32]{0:T(128)} %fill.1, s32[32]{0:T(128)} %length.1, bf16[5,8,4096]{2,1,0:T(8,128)(2,1)} %feat_hbm.1, bf16[1024,1024]{1,0:T(8,128)(2,1)} %bitcast.2, bf16[32,64,512]{2,1,0:T(8,128)(2,1)} %lk_hbm.1, ...), custom_call_target="tpu_custom_call" | custom-call | tf_op jit(solution)/shard_map/layer/pallas_call | solution.py:461
  73.2 2.0 %copy.17 = bf16[32,5,1024]{2,0,1:T(8,128)(2,1)} copy(bf16[32,5,1024]{2,1,0:T(8,128)(2,1)} %get-tuple-element.4) | data formatting | bytes 655360 | tf_op jit(solution)/shard_map/layer/pallas_call | solution.py:461
  75.1 1.5 %copy.21 = bf16[32,1024]{1,0:T(8,128)(2,1)} copy(bf16[32,1024]{1,0:T(8,128)(2,1)} %get-tuple-element.13) | data formatting | bytes 131072
  76.6 1.6 %copy.22 = bf16[32,4,512]{2,1,0:T(4,128)(2,1)} copy(bf16[32,4,512]{2,1,0:T(4,128)(2,1)} %get-tuple-element.14) | data formatting | bytes 262144
  78.2 1.6 %copy.23 = bf16[32,4,512]{2,1,0:T(4,128)(2,1)} copy(bf16[32,4,512]{2,1,0:T(4,128)(2,1)} %get-tuple-element.15) | data formatting | bytes 262144

commit v2 on v1

--- a/solution.py
+++ b/solution.py
@@ -16,6 +16,8 @@
 ROWS = 8
 KEYS = 112
 UNITS = 12
+DIRECT = 8
+ORDER = (0, 1, 2, 8, 9, 3, 10, 11, 4, 5, 6, 7)
 EPS = 1e-05
 MASKED = -1e30
 F32 = jnp.float32
@@ -57,6 +59,7 @@
     held,
     perm,
     rows,
+    frames_first,
     xp,
     x,
     n,
@@ -72,6 +75,8 @@
     down,
     down_out,
     down_in,
+    k_half,
+    v_half,
     l_sem,
     g_send,
     g_recv,
@@ -81,6 +86,8 @@
     c_recv,
     f_send,
     f_recv,
+    z_send,
+    z_recv,
     e_send,
     e_recv,
 ):
@@ -110,6 +117,9 @@
         )
 
     flipped = d + 32 * (1 - 2 * xl)
+    over = lax.div(flipped, 2)
+    z_up = dev(d - z + lax.rem(z + 1, 8), f, m)
+    z_down = dev(d - z + lax.rem(z + 7, 8), f, m)
     up_d = xl * 32 + lax.rem(y + 1, 4) * 8 + z
     down_d = xl * 32 + lax.rem(y + 3, 4) * 8 + z
     cross_dev = dev(flipped, 1 - f, m)
@@ -129,13 +139,12 @@
     load_lk = load(UNITS + 2, lk_hbm, keys.at[:, pl.ds(MEM, LEFT), :])
     load_lv = load(UNITS + 3, lv_hbm, values.at[:, pl.ds(MEM, LEFT), :])
     load_feat.start()
-    for c in loads[:4]:
-        c.start()
+    loads[0].start()
     load_mem.start()
+    for u in ORDER[1:]:
+        loads[u].start()
     load_lk.start()
     load_lv.start()
-    for c in loads[4:]:
-        c.start()
 
     barrier = pltpu.get_barrier_semaphore()
 
@@ -154,67 +163,19 @@
     def quad(e):
         s = lax.rem(slot + e, 8)
         rr = lax.div(s, 2)
-        return rr, dev(2 * k + lax.div(rr, 2), lax.rem(rr, 2), lax.rem(s, 2))
+        return rr, dev(2 * over + lax.div(rr, 2), lax.rem(rr, 2), lax.rem(s, 2))
 
     def greet_quad(e, _):
         greet(quad(e)[1])
         return 0
 
-    lax.fori_loop(1, 8, greet_quad, 0)
+    lax.fori_loop(0, 8, greet_quad, 0)
     greet(cross_dev)
     for to in ring:
         greet(to)
     greet(sibling)
-    pl.semaphore_wait(barrier, 16 + 7 + 1 + 3 + 1)
-
-    def first_copy(j):
-        t = 2 * lax.rem(j + lax.div(k, 2), 16) + (1 - m)
-        return remote(
-            feat.at[:, :, pl.ds(pl.multiple_of(t * 128, 128), 128)],
-            gath.at[lax.div(k, 2)],
-            g_send.at[j],
-            g_recv.at[lax.div(k, 2)],
-            dev(2 * t + odd, f, lax.rem(k, 2)),
-        )
-
-    def send_first(j, _):
-        first_copy(j).start()
-        return 0
-
-    load_feat.wait()
-    lax.fori_loop(0, 16, send_first, 0)
-
-    def piece(ref, u, c):
-        return ref.at[u, pl.ds(pl.multiple_of(c * 128, 128), 128), :]
-
-    other = lax.rem(color + 2, 4)
-
-    def cross_copy(u):
-        return remote(
-            piece(own, u, other), piece(got, u, other), c_send.at[u], c_recv.at[u], cross_dev
-        )
-
-    def forward_copy(u, i):
-        return remote(
-            piece(got, u, color), piece(got, u, color), f_send.at[u, i], f_recv.at[u, i], ring[i]
-        )
-
-    def wait_got(u, c, sem):
-        pltpu.make_async_copy(piece(got, u, c), piece(got, u, c), sem).wait()
-
-    def forward(u):
-        wait_got(u, color, c_recv.at[u])
-        for i in range(3):
-            forward_copy(u, i).start()
-
-    def ready(u):
-        wait_got(u, lax.rem(color + 2, 4), f_recv.at[u, 0])
-        wait_got(u, lax.rem(color + 3, 4), f_recv.at[u, 1])
-        wait_got(u, lax.rem(color + 1, 4), f_recv.at[u, 2])
-
-    for u in range(UNITS):
-        loads[u].wait()
-        cross_copy(u).start()
+    greet(z_up)
+    greet(z_down)
 
     def build_perm(s, _):
         at = lax.broadcasted_iota(jnp.int32, (128, 1024), 0)
@@ -229,7 +190,118 @@
     at = lax.broadcasted_iota(jnp.int32, (STR * ROWS, STR * FRAMES), 0)
     col = lax.broadcasted_iota(jnp.int32, (STR * ROWS, STR * FRAMES), 1)
     rows[...] = jnp.where(col == (at & 7) * STR + (at >> 3), 1.0, 0.0).astype(BF16)
+    at = lax.broadcasted_iota(jnp.int32, (STR * FRAMES, STR * ROWS), 0)
+    col = lax.broadcasted_iota(jnp.int32, (STR * FRAMES, STR * ROWS), 1)
+    frames_first[...] = jnp.where(col == (at & 31) * ROWS + (at >> 5), 1.0, 0.0).astype(BF16)
     att[...] = jnp.zeros_like(att)
+
+    mine = pl.ds(pl.multiple_of(f * 512, 512), 512)
+    theirs = pl.ds(pl.multiple_of((1 - f) * 512, 512), 512)
+
+    def own_half(u, place):
+        def memory_rows(c, _):
+            at = pl.ds(pl.multiple_of(c * 256, 256), 256)
+            place[at, :] = dot(memory[at, mine], own[u])
+            return 0
+
+        lax.fori_loop(0, 4, memory_rows, 0)
+
+    loads[0].wait()
+    load_mem.wait()
+    own_half(0, k_half)
+    pl.semaphore_wait(barrier, 16 + 8 + 1 + 3 + 1 + 2)
+
+    def first_copy(j):
+        t = 2 * lax.rem(j + lax.div(over, 2), 16) + (1 - m)
+        return remote(
+            feat.at[:, :, pl.ds(pl.multiple_of(t * 128, 128), 128)],
+            gath.at[lax.div(k, 2)],
+            g_send.at[j],
+            g_recv.at[lax.div(k, 2)],
+            dev(lax.rem(2 * t + 32, 64) + odd, f, lax.rem(k, 2)),
+        )
+
+    def send_first(j, _):
+        first_copy(j).start()
+        return 0
+
+    load_feat.wait()
+    lax.fori_loop(0, 16, send_first, 0)
+
+    def piece(ref, u, c):
+        return ref.at[u, pl.ds(pl.multiple_of(c * 128, 128), 128), :]
+
+    def eighth(ref, u, step):
+        c = lax.rem(z + 8 + step, 8)
+        return ref.at[u, pl.ds(pl.multiple_of(c * 64, 64), 64), :]
+
+    def sixteenth(ref, u, step, half):
+        c = lax.rem(z + 8 + step, 8)
+        return ref.at[u, pl.ds(pl.multiple_of(c * 64 + 32 * half, 32), 32), :]
+
+    other = lax.rem(color + 2, 4)
+
+    def cross_copy(u):
+        if u < DIRECT:
+            src, dst = piece(own, u, other), piece(got, u, other)
+        else:
+            src, dst = eighth(own, u, 0), eighth(got, u, 0)
+        return remote(src, dst, c_send.at[u], c_recv.at[u], cross_dev)
+
+    def forward_copy(u, i):
+        return remote(
+            piece(got, u, color), piece(got, u, color), f_send.at[u, i], f_recv.at[u, i], ring[i]
+        )
+
+    def ring_copy(u, step, way):
+        sign = 1 - 2 * way
+        if step < 3:
+            at = eighth(got, u, -sign * step)
+        else:
+            at = sixteenth(got, u, -sign * step, way)
+        sems = z_send.at[u - DIRECT, step, way], z_recv.at[u - DIRECT, step, way]
+        return remote(at, at, *sems, (z_up, z_down)[way])
+
+    def arrived(ref, sem):
+        pltpu.make_async_copy(ref, ref, sem).wait()
+
+    def forward(u):
+        arrived(piece(got, u, color), c_recv.at[u])
+        for i in range(3):
+            forward_copy(u, i).start()
+
+    def ring_arrived(u, step, way):
+        sign = 1 - 2 * way
+        if step < 3:
+            at = eighth(got, u, -sign * (step + 1))
+        else:
+            at = sixteenth(got, u, -sign * (step + 1), way)
+        arrived(at, z_recv.at[u - DIRECT, step, way])
+
+    def circulate(u, step):
+        for way in range(2):
+            if step > 0:
+                ring_arrived(u, step - 1, way)
+            elif way == 0:
+                arrived(eighth(got, u, 0), c_recv.at[u])
+            ring_copy(u, step, way).start()
+
+    def ready(u):
+        if u < DIRECT:
+            for i, c in enumerate((2, 3, 1)):
+                arrived(piece(got, u, lax.rem(color + c, 4)), f_recv.at[u, i])
+        else:
+            for way in range(2):
+                ring_arrived(u, 3, way)
+
+    def across(units):
+        for u in units:
+            if u > 0:
+                loads[u].wait()
+            cross_copy(u).start()
+
+    across(ORDER[:2])
+    own_half(1, v_half)
 
     def wait_first(j, _):
         pltpu.make_async_copy(gath.at[j], gath.at[j], g_recv.at[j]).wait()
@@ -248,9 +320,9 @@
         second_copy(e).start()
         return 0
 
-    lax.fori_loop(1, 8, send_second, 0)
-    held[slot] = blocks[r]
-
+    lax.fori_loop(0, 8, send_second, 0)
+
+    across(ORDER[2:])
     forward(0)
     forward(1)
 
@@ -259,7 +331,7 @@
         pltpu.make_async_copy(held.at[s], held.at[s], h_recv.at[s]).wait()
         return 0
 
-    lax.fori_loop(1, 8, wait_second, 0)
+    lax.fori_loop(0, 8, wait_second, 0)
     for s in range(8):
         xp[:, pl.ds(128 * s, 128)] = held[s].reshape(STR * FRAMES, 128)
     for h in range(2):
@@ -282,20 +354,17 @@
         split_norm(v.reshape(32, 1024), c)
         return 0
 
-    lax.fori_loop(0, 8, first_norm, 0)
+    lax.fori_loop(0, 8, first_norm, 0, unroll=4)
     forward(2)
-
-    load_mem.wait()
+    circulate(8, 0)
+
     load_lk.wait()
     load_lv.wait()
 
-    mine = pl.ds(pl.multiple_of(f * 512, 512), 512)
-    theirs = pl.ds(pl.multiple_of((1 - f) * 512, 512), 512)
-
-    def project(u, place, center):
+    def project(u, half, place, center):
         def memory_rows(c, _):
             at = pl.ds(pl.multiple_of(c * 256, 256), 256)
-            sums = dot(memory[at, mine], own[u]) + dot(memory[at, theirs], got[u])
+            sums = half[at, :] + dot(memory[at, theirs], got[u])
             place[pl.ds(c * 8, 8), pl.ds(0, MEM), :] = sums.astype(BF16).reshape(8, MEM, 512)
             return 0
 
@@ -313,10 +382,12 @@
         lax.fori_loop(0, 4, group_rows, 0)
 
     ready(0)
-    project(0, keys, center_k)
+    project(0, k_half, keys, center_k)
+    circulate(9, 0)
+    ready(1)
+    project(1, v_half, values, center_v)
     forward(3)
-    ready(1)
-    project(1, values, center_v)
+    circulate(8, 1)
     ready(2)
     q[...] = (
         (dot(n[f], own[2]) + dot(n[1 - f], got[2])).astype(BF16).astype(F32) * (HD**-0.5)
@@ -331,37 +402,58 @@
     )
     queries = FRAMES + 1
 
-    def attend(s):
-        q8 = q[s]
-        spread = jnp.concatenate(
-            [jnp.broadcast_to(q8[i : i + 1], (heads, 512)) * head_mask for i in range(queries)],
-            axis=0,
-        ).astype(BF16)
-        scores = lax.dot_general(
-            spread, keys[s], (((1,), (1,)), ((), ())), preferred_element_type=F32
-        )
-        row = lax.broadcasted_iota(jnp.int32, scores.shape, 0)
-        col = lax.broadcasted_iota(jnp.int32, scores.shape, 1)
-        seen_mem = (col >= MEM - fill[s]) & (col < MEM) & (row < FRAMES * heads)
-        seen_left = (col >= MEM + LEFT - length[s]) & (col < MEM + LEFT + FRAMES)
-        scores = jnp.where(seen_mem | seen_left, scores, MASKED)
-        e = jnp.exp(scores - jnp.max(scores, axis=-1, keepdims=True))
-        probs = (e / jnp.sum(e, axis=-1, keepdims=True)).astype(BF16)
-        mixed = dot(probs, values[s]).reshape(queries, heads, 512)
-        att[s, pl.ds(0, queries), :] = jnp.sum(mixed * head_mask[None], axis=1)
-
-    def attend_block(b, _):
-        forward(4 + b)
-
-        def pair(i, _):
-            attend(b * 8 + 2 * i)
-            attend(b * 8 + 2 * i + 1)
+    width = 4
+
+    def attend(first):
+        streams = [first + i for i in range(width)]
+        probs = []
+        scored = []
+        for s in streams:
+            q8 = q[s]
+            spread = jnp.concatenate(
+                [
+                    jnp.broadcast_to(q8[i : i + 1], (heads, 512)) * head_mask
+                    for i in range(queries)
+                ],
+                axis=0,
+            ).astype(BF16)
+            scored.append(
+                lax.dot_general(
+                    spread, keys[s], (((1,), (1,)), ((), ())), preferred_element_type=F32
+                )
+            )
+        row = lax.broadcasted_iota(jnp.int32, (queries * heads, KEYS), 0)
+        col = lax.broadcasted_iota(jnp.int32, (queries * heads, KEYS), 1)
+        in_mem = (col < MEM) & (row < FRAMES * heads)
+        in_rest = col < MEM + LEFT + FRAMES
+        for s, scores in zip(streams, scored):
+            seen_mem = (col >= MEM - fill[s]) & in_mem
+            seen_left = (col >= MEM + LEFT - length[s]) & in_rest
+            scores = jnp.where(seen_mem | seen_left, scores, MASKED)
+            e = jnp.exp(scores - jnp.max(scores, axis=-1, keepdims=True))
+            probs.append((e / jnp.sum(e, axis=-1, keepdims=True)).astype(BF16))
+        for s, p in zip(streams, probs):
+            mixed = dot(p, values[s]).reshape(queries, heads, 512)
+            att[s, pl.ds(0, queries), :] = jnp.sum(mixed * head_mask[None], axis=1)
+
+    def attend_block(b):
+        def few(i, _):
+            attend(b * 8 + width * i)
             return 0
 
-        lax.fori_loop(0, 4, pair, 0)
-        return 0
-
-    lax.fori_loop(0, 4, attend_block, 0)
+        lax.fori_loop(0, 8 // width, few, 0)
+
+    circulate(9, 1)
+    circulate(10, 0)
+    attend_block(0)
+    circulate(8, 2)
+    circulate(11, 0)
+    attend_block(1)
+    circulate(9, 2)
+    attend_block(2)
+    circulate(10, 1)
+    forward(4)
+    attend_block(3)
 
     def exchange(src, dst, i):
         return remote(src, dst, e_send.at[i], e_recv.at[i], sibling)
@@ -369,10 +461,13 @@
     ready(3)
     a = att[...].reshape(STR * ROWS, 512).astype(BF16)
     part[f] = dot(a, own[3]).astype(BF16)
+    exchange(part.at[f], part_in.at[f], 0).start()
     part[1 - f] = dot(a, got[3]).astype(BF16)
-    first = exchange(part, part_in, 0)
-    first.start()
-    first.wait()
+    exchange(part.at[1 - f], part_in.at[1 - f], 1).start()
+    circulate(8, 3)
+    circulate(11, 1)
+    exchange(part.at[f], part_in.at[f], 0).wait()
+    exchange(part.at[1 - f], part_in.at[1 - f], 1).wait()
 
     def second_norm(c, _):
         at = pl.ds(pl.multiple_of(c * 32, 32), 32)
@@ -382,40 +477,55 @@
         split_norm(normalized(v), c)
         return 0
 
-    lax.fori_loop(0, 8, second_norm, 0)
+    lax.fori_loop(0, 8, second_norm, 0, unroll=4)
+    circulate(9, 3)
+    forward(5)
     mem_next[...] = jnp.tanh(x[...].reshape(STR, ROWS, 1024)[:, FRAMES, :]).astype(BF16)
 
-    down[...] = jnp.zeros_like(down)
-
-    def hidden_block(j, _):
-        @pl.when(j < 2)
-        def _():
-            forward(8 + 2 * j)
-            forward(9 + 2 * j)
-
-        ready(4 + 2 * j)
-        sums = dot(n[f], own[4 + 2 * j]) + dot(n[1 - f], got[4 + 2 * j])
+    def hidden_block(u, pumps):
+        ready(u)
+        sums = dot(n[f], own[u]) + dot(n[1 - f], got[u])
         hid = jax.nn.gelu(sums, approximate=True).astype(BF16)
-        ready(5 + 2 * j)
-        down[f] += dot(hid, own[5 + 2 * j])
-        down[1 - f] += dot(hid, got[5 + 2 * j])
-        return 0
-
-    lax.fori_loop(0, 4, hidden_block, 0)
-    down_out[...] = down[...].astype(BF16)
-    last = exchange(down_out, down_in, 1)
-    last.start()
-    last.wait()
+        for pump in pumps:
+            pump()
+        ready(u + 1)
+        return hid
+
+    def pump(u, step=None):
+        return functools.partial(forward, u) if step is None else functools.partial(circulate, u, step)
+
+    hid = hidden_block(8, (pump(10, 2),))
+    down[f] = dot(hid, own[9])
+    down[1 - f] = dot(hid, got[9])
+    circulate(11, 2)
+    forward(6)
+    hid = hidden_block(4, (pump(10, 3),))
+    down[f] += dot(hid, own[5])
+    down[1 - f] += dot(hid, got[5])
+    circulate(11, 3)
+    forward(7)
+    hid = hidden_block(10, ())
+    down[f] += dot(hid, own[11])
+    down[1 - f] += dot(hid, got[11])
+    hid = hidden_block(6, ())
+    down_out[f] = (down[f] + dot(hid, own[7])).astype(BF16)
+    exchange(down_out.at[f], down_in.at[f], 2).start()
+    down_out[1 - f] = (down[1 - f] + dot(hid, got[7])).astype(BF16)
+    exchange(down_out.at[1 - f], down_in.at[1 - f], 3).start()
+    exchange(down_out.at[f], down_in.at[f], 2).wait()
+    exchange(down_out.at[1 - f], down_in.at[1 - f], 3).wait()
 
     def third_norm(c, _):
         at = pl.ds(pl.multiple_of(c * 32, 32), 32)
         summed = [down_out[h, at, :].astype(F32) + down_in[h, at, :].astype(F32) for h in range(2)]
         v = x[at, :] + jnp.concatenate(summed, axis=1)
-        w = (normalized(v) * gain[...]).reshape(4, ROWS, 1024)
-        out[pl.ds(c * 4, 4), :, :] = w[:, :FRAMES, :].astype(BF16)
-        return 0
-
-    lax.fori_loop(0, 8, third_norm, 0)
+        split_norm(normalized(v) * gain[...], c)
+        return 0
+
+    lax.fori_loop(0, 8, third_norm, 0, unroll=4)
+    for h in range(2):
+        placed = dot(frames_first[...], n[h]).astype(BF16)
+        out[:, :, pl.ds(512 * h, 512)] = placed.reshape(FRAMES, STR, 512)
 
     def drain_first(j, _):
         first_copy(j).wait_send()
@@ -427,15 +537,34 @@
         second_copy(e).wait_send()
         return 0
 
-    lax.fori_loop(1, 8, drain_second, 0)
-
-    def drain(u, _):
+    lax.fori_loop(0, 8, drain_second, 0)
+
+    for u in range(UNITS):
         cross_copy(u).wait_send()
-        for i in range(3):
-            forward_copy(u, i).wait_send()
-        return 0
-
-    lax.fori_loop(0, UNITS, drain, 0)
+        if u < DIRECT:
+            for i in range(3):
+                forward_copy(u, i).wait_send()
+        else:
+            for step in range(4):
+                for way in range(2):
+                    ring_copy(u, step, way).wait_send()
+
+
+def hand_over(*refs):
+    given, held, results, into, out_of = refs[:4], refs[4:8], refs[8:12], refs[12], refs[13]
+    arrive = [
+        pltpu.make_async_copy(*pair, into.at[i]) for i, pair in enumerate(zip(given, results))
+    ]
+    leave = [
+        pltpu.make_async_copy(*pair, out_of.at[i]) for i, pair in enumerate(zip(results, held))
+    ]
+    for copy in arrive:
+        copy.start()
+    for i in range(4):
+        arrive[i].wait()
+        leave[i].start()
+    for copy in leave:
+        copy.wait()
 
 
 def shards(
@@ -455,18 +584,19 @@
 ):
     memory = memory_bank.reshape(STR * MEM, 1024)
     smem = pl.BlockSpec(memory_space=pltpu.SMEM)
-    hbm = pl.BlockSpec(memory_space=pl.ANY)
+    hbm = pl.BlockSpec(memory_space=pltpu.HBM)
     vmem = pl.BlockSpec(memory_space=pltpu.VMEM)
     dma = pltpu.SemaphoreType.DMA
-    return pl.pallas_call(
+    shapes = (
+        jax.ShapeDtypeStruct((FRAMES, STR, 1024), BF16),
+        jax.ShapeDtypeStruct((STR, 1024), BF16),
+        jax.ShapeDtypeStruct((STR, GROUP, 512), BF16),
+        jax.ShapeDtypeStruct((STR, GROUP, 512), BF16),
+    )
+    results = pl.pallas_call(
         kernel,
         name="layer",
-        out_shape=(
-            jax.ShapeDtypeStruct((STR, FRAMES, 1024), BF16),
-            jax.ShapeDtypeStruct((STR, 1024), BF16),
-            jax.ShapeDtypeStruct((STR, GROUP, 512), BF16),
-            jax.ShapeDtypeStruct((STR, GROUP, 512), BF16),
-        ),
+        out_shape=shapes,
         in_specs=[smem] * 2 + [hbm] * 10 + [vmem],
         out_specs=(vmem,) * 4,
         scratch_shapes=[
@@ -476,6 +606,7 @@
             pltpu.VMEM((8, FRAMES, STR, 128), BF16),
             pltpu.VMEM((1024, 1024), BF16),
             pltpu.VMEM((STR * ROWS, STR * FRAMES), BF16),
+            pltpu.VMEM((STR * FRAMES, STR * ROWS), BF16),
             pltpu.VMEM((STR * FRAMES, 1024), BF16),
             pltpu.VMEM((STR * ROWS, 1024), F32),
             pltpu.VMEM((2, STR * ROWS, 512), BF16),
@@ -491,6 +622,8 @@
             pltpu.VMEM((2, STR * ROWS, 512), F32),
             pltpu.VMEM((2, STR * ROWS, 512), BF16),
             pltpu.VMEM((2, STR * ROWS, 512), BF16),
+            pltpu.VMEM((STR * MEM, 512), F32),
+            pltpu.VMEM((STR * MEM, 512), F32),
             dma((UNITS + 4,)),
             dma((16,)),
             dma((16,)),
@@ -498,13 +631,15 @@
             dma((8,)),
             dma((UNITS,)),
             dma((UNITS,)),
-            dma((UNITS, 3)),
-            dma((UNITS, 3)),
-            dma((2,)),
-            dma((2,)),
+            dma((DIRECT, 3)),
+            dma((DIRECT, 3)),
+            dma((UNITS - DIRECT, 4, 2)),
+            dma((UNITS - DIRECT, 4, 2)),
+            dma((4,)),
+            dma((4,)),
         ],
         compiler_params=pltpu.CompilerParams(
-            collective_id=0, has_side_effects=True, vmem_limit_bytes=60 * 1024 * 1024
+            collective_id=0, has_side_effects=True, vmem_limit_bytes=62_600_000
         ),
     )(
         memory_fill,
@@ -521,6 +656,16 @@
         w_down,
         out_gain.reshape(1, 1024),
     )
+    layer_out, memory_next, center_keys, center_values = pl.pallas_call(
+        hand_over,
+        name="hand_over",
+        out_shape=shapes,
+        in_specs=[hbm] * 4,
+        out_specs=(hbm,) * 4,
+        scratch_shapes=[pltpu.VMEM(v.shape, v.dtype) for v in shapes] + [dma((4,)), dma((4,))],
+        compiler_params=pltpu.CompilerParams(vmem_limit_bytes=62_600_000),
+    )(*results)
+    return jnp.transpose(layer_out, (1, 0, 2)), memory_next, center_keys, center_values
 
 
 def solution(mesh):

time: 80.1 us -> 68.1 us (0.85)
  local copies, waits for them, and re-layouts: 6.67 us -> 0 us
  Pallas kernels: 72.5 us -> 67.4 us
    pallas_call x1 -> x2, Pallas kernels: 72.5 us -> 67.4 us  [the longest x1 65.5 us: shards(): pl.pallas_call(kernel, name='layer', out_shape=shapes, in_specs=[smem] *...]
    unnamed x3 -> x0, local copies, waits for them, and re-layouts: 4.68 us -> none
    pallas_call x1 -> x0, local copies, waits for them, and re-layouts: 1.99 us -> none  [shards(): pl.pallas_call(kernel, name='layer', out_shape=(jax.ShapeDtypeStruct((STR...]
where the time goes in v2:
time: 68.1 us; the launch traced here: 68 us
  Pallas kernels  67.4 us (99%)
    pallas_call x1, Pallas kernels, shards(): pl.pallas_call(kernel, name='layer', out_shape=shapes, in_specs=[smem] *...  65.5 us
    pallas_call x1, Pallas kernels, shards(): pl.pallas_call(hand_over, name='hand_over', out_shape=shapes, in_specs=[h...  1.87 us

profile of v2, /device:TPU:1, one launch (start us, length us, event | category | flops | bytes accessed | tf_op | source)
XLA Modules:
  0.0 68.0 jit_solution(7774872980080666371)
XLA Ops:
  0.6 65.5 %layer.1 = (bf16[5,32,1024]{2,1,0:T(8,128)(2,1)}, bf16[32,1024]{1,0:T(8,128)(2,1)}, bf16[32,4,512]{2,1,0:T(4,128)(2,1)}, bf16[32,4,512]{2,1,0:T(4,128)(2,1)}) custom-call(s32[32]{0:T(128)} %fill.1, s32[32]{0:T(128)} %length.1, bf16[5,8,4096]{2,1,0:T(8,128)(2,1)} %feat_hbm.1, bf16[1024,1024]{1,0:T(8,128)(2,1)} %bitcast.3, bf16[32,64,512]{2,1,0:T(8,128)(2,1)} %lk_hbm.1, ...), custom_call_target="tpu_custom_call" | custom-call | tf_op jit(solution)/shard_map/layer/pallas_call | solution.py:596
  66.1 1.9 %hand_over.1 = (bf16[5,32,1024]{2,1,0:T(8,128)(2,1)}, bf16[32,1024]{1,0:T(8,128)(2,1)}, bf16[32,4,512]{2,1,0:T(4,128)(2,1)}, bf16[32,4,512]{2,1,0:T(4,128)(2,1)}) custom-call(bf16[5,32,1024]{2,1,0:T(8,128)(2,1)} %get-tuple-element.12.refs_0_, bf16[32,1024]{1,0:T(8,128)(2,1)} %get-tuple-element.13.refs_1_, bf16[32,4,512]{2,1,0:T(4,128)(2,1)} %get-tuple-element.14.refs_2_, ...), custom_call_target="tpu_custom_call" | custom-call | tf_op jit(solution)/shard_map/hand_over/pallas_call | solution.py:659

commit v3 on v2

--- a/solution.py
+++ b/solution.py
@@ -16,8 +16,63 @@
 ROWS = 8
 KEYS = 112
 UNITS = 12
-DIRECT = 8
-ORDER = (0, 1, 2, 8, 9, 3, 10, 11, 4, 5, 6, 7)
+KIND = (1, 1, 1, 1, 2, 2, 1, 0, 2, 0, 0, 0)
+ORDER = (1, 0, 2, 6, 3, 4, 5, 8, 7, 10, 11, 9)
+EARLY = 4
+BLOCKS = (3, 1, 0, 2)
+STEPS = (
+    ("own_v", 0),
+    ("forward", 1),
+    ("turn", 0),
+    ("forward", 0),
+    ("forward", 2),
+    ("second", 1),
+    ("forward", 6),
+    ("relay", 0),
+    ("second", 0),
+    ("forward", 3),
+    ("norm", 0),
+    ("second", 2),
+    ("circulate", 4, 0),
+    ("second", 6),
+    ("mem_v", 0),
+    ("circulate", 5, 0),
+    ("group_v", 0),
+    ("second", 3),
+    ("circulate", 8, 0),
+    ("mem_k", 0),
+    ("circulate", 4, 1),
+    ("group_k", 0),
+    ("forward", 7),
+    ("circulate", 5, 1),
+    ("query", 0),
+    ("attend", 0),
+    ("circulate", 8, 1),
+    ("attend", 1),
+    ("forward", 10),
+    ("circulate", 4, 2),
+    ("attend", 2),
+    ("circulate", 5, 2),
+    ("attend", 3),
+    ("forward", 11),
+    ("output", 0),
+    ("circulate", 8, 2),
+    ("circulate", 4, 3),
+    ("norm_two", 0),
+    ("forward", 9),
+    ("next", 0),
+    ("circulate", 5, 3),
+    ("hidden", 3),
+    ("circulate", 8, 3),
+    ("down", 3),
+    ("hidden", 1),
+    ("down", 1),
+    ("hidden", 0),
+    ("down", 0),
+    ("hidden", 2),
+    ("down", 2),
+    ("finish", 0),
+)
 EPS = 1e-05
 MASKED = -1e30
 F32 = jnp.float32
@@ -77,16 +132,18 @@
     down_in,
     k_half,
     v_half,
+    out_vm,
+    mem_vm,
+    ck_vm,
+    cv_vm,
+    o_sem,
     l_sem,
-    g_send,
+    sent,
     g_recv,
-    h_send,
     h_recv,
-    c_send,
     c_recv,
-    f_send,
+    s_recv,
     f_recv,
-    z_send,
     z_recv,
     e_send,
     e_recv,
@@ -100,7 +157,6 @@
     k = lax.div(d, 2)
     odd = lax.rem(d, 2)
     r = odd * 2 + f
-    slot = r * 2 + m
     color = lax.rem(y + 2 * xl, 4)
 
     def dev(dd, ff, mm):
@@ -120,11 +176,19 @@
     over = lax.div(flipped, 2)
     z_up = dev(d - z + lax.rem(z + 1, 8), f, m)
     z_down = dev(d - z + lax.rem(z + 7, 8), f, m)
+    z_pair = dev(d + 1 - 2 * odd, f, m)
     up_d = xl * 32 + lax.rem(y + 1, 4) * 8 + z
     down_d = xl * 32 + lax.rem(y + 3, 4) * 8 + z
     cross_dev = dev(flipped, 1 - f, m)
     ring = (dev(flipped, f, m), dev(up_d, f, m), dev(down_d, f, m))
     sibling = dev(d, f, 1 - m)
+
+    write = [
+        pltpu.make_async_copy(src, dst, o_sem.at[i])
+        for i, (src, dst) in enumerate(
+            ((out_vm, out), (mem_vm, mem_next), (ck_vm, center_k), (cv_vm, center_v))
+        )
+    ]
 
     def load(i, src, dst):
         return pltpu.make_async_copy(src, dst, l_sem.at[i])
@@ -141,8 +205,9 @@
     load_feat.start()
     loads[0].start()
     load_mem.start()
-    for u in ORDER[1:]:
-        loads[u].start()
+    for u in ORDER:
+        if u > 0:
+            loads[u].start()
     load_lk.start()
     load_lv.start()
 
@@ -161,26 +226,26 @@
     lax.fori_loop(0, 16, greet_sources, 0)
 
     def quad(e):
-        s = lax.rem(slot + e, 8)
-        rr = lax.div(s, 2)
-        return rr, dev(2 * over + lax.div(rr, 2), lax.rem(rr, 2), lax.rem(s, 2))
+        rr = lax.rem(r + e, 4)
+        return rr, dev(2 * over + lax.div(rr, 2), lax.rem(rr, 2), m)
 
     def greet_quad(e, _):
         greet(quad(e)[1])
         return 0
 
-    lax.fori_loop(0, 8, greet_quad, 0)
+    lax.fori_loop(0, 4, greet_quad, 0)
     greet(cross_dev)
     for to in ring:
         greet(to)
     greet(sibling)
     greet(z_up)
     greet(z_down)
+    greet(z_pair)
 
     def build_perm(s, _):
         at = lax.broadcasted_iota(jnp.int32, (128, 1024), 0)
         col = lax.broadcasted_iota(jnp.int32, (128, 1024), 1)
-        want = (at >> 3) * 64 + lax.rem(s, 2) * 32 + lax.div(s, 2) * 8 + (at & 7)
+        want = (at >> 3) * 64 + lax.div(s, 4) * 32 + lax.rem(s, 4) * 8 + (at & 7)
         perm[pl.ds(pl.multiple_of(s * 128, 128), 128), :] = jnp.where(
             col == want, 1.0, 0.0
         ).astype(BF16)
@@ -209,15 +274,15 @@
     loads[0].wait()
     load_mem.wait()
     own_half(0, k_half)
-    pl.semaphore_wait(barrier, 16 + 8 + 1 + 3 + 1 + 2)
+    pl.semaphore_wait(barrier, 16 + 4 + 1 + 3 + 1 + 2 + 1)
 
     def first_copy(j):
         t = 2 * lax.rem(j + lax.div(over, 2), 16) + (1 - m)
         return remote(
             feat.at[:, :, pl.ds(pl.multiple_of(t * 128, 128), 128)],
             gath.at[lax.div(k, 2)],
-            g_send.at[j],
-            g_recv.at[lax.div(k, 2)],
+            sent.at[0],
+            g_recv.at[0],
             dev(lax.rem(2 * t + 32, 64) + odd, f, lax.rem(k, 2)),
         )
 
@@ -228,71 +293,82 @@
     load_feat.wait()
     lax.fori_loop(0, 16, send_first, 0)
 
-    def piece(ref, u, c):
-        return ref.at[u, pl.ds(pl.multiple_of(c * 128, 128), 128), :]
-
-    def eighth(ref, u, step):
-        c = lax.rem(z + 8 + step, 8)
-        return ref.at[u, pl.ds(pl.multiple_of(c * 64, 64), 64), :]
-
-    def sixteenth(ref, u, step, half):
-        c = lax.rem(z + 8 + step, 8)
-        return ref.at[u, pl.ds(pl.multiple_of(c * 64 + 32 * half, 32), 32), :]
-
-    other = lax.rem(color + 2, 4)
+    def part_of(ref, u, at, count=64):
+        return ref.at[u, pl.ds(pl.multiple_of(at, 32), count), :]
+
+    def direct(c, parity):
+        return lax.rem(c + 8, 4) * 128 + parity * 64
+
+    def around(step):
+        return lax.rem(z + 8 + step, 8) * 64
+
+    zp = lax.rem(z, 2)
+
+    def mine_of(u, c):
+        if KIND[u] == 0:
+            return part_of(got, u, direct(c, 0), 128)
+        return part_of(got, u, direct(c, zp) if KIND[u] == 1 else around(0))
 
     def cross_copy(u):
-        if u < DIRECT:
-            src, dst = piece(own, u, other), piece(got, u, other)
+        if KIND[u] == 0:
+            at, count = direct(color + 2, 0), 128
         else:
-            src, dst = eighth(own, u, 0), eighth(got, u, 0)
-        return remote(src, dst, c_send.at[u], c_recv.at[u], cross_dev)
-
-    def forward_copy(u, i):
+            at, count = direct(color + 2, zp) if KIND[u] == 1 else around(0), 64
         return remote(
-            piece(got, u, color), piece(got, u, color), f_send.at[u, i], f_recv.at[u, i], ring[i]
+            part_of(own, u, at, count),
+            part_of(got, u, at, count),
+            sent.at[3 + u],
+            c_recv.at[u],
+            cross_dev,
         )
 
+    def swap_copy(u):
+        ref = part_of(got, u, direct(color, zp))
+        return remote(ref, ref, sent.at[3 + u], s_recv.at[KIND[:u].count(1)], z_pair)
+
+    def forward_copy(u, i, late):
+        ref = part_of(got, u, direct(color, 1 - zp)) if late else mine_of(u, color)
+        return remote(ref, ref, sent.at[3 + u], f_recv.at[u], ring[i])
+
+    def ring_place(u, hop, way, half):
+        at = around(hop * (2 * way - 1))
+        return part_of(got, u, at + 32 * way, 32) if half else part_of(got, u, at)
+
     def ring_copy(u, step, way):
-        sign = 1 - 2 * way
-        if step < 3:
-            at = eighth(got, u, -sign * step)
-        else:
-            at = sixteenth(got, u, -sign * step, way)
-        sems = z_send.at[u - DIRECT, step, way], z_recv.at[u - DIRECT, step, way]
-        return remote(at, at, *sems, (z_up, z_down)[way])
+        ref = ring_place(u, step, way, step == 3)
+        return remote(ref, ref, sent.at[3 + u], z_recv.at[KIND[:u].count(2), step], (z_up, z_down)[way])
 
     def arrived(ref, sem):
         pltpu.make_async_copy(ref, ref, sem).wait()
 
     def forward(u):
-        arrived(piece(got, u, color), c_recv.at[u])
+        arrived(mine_of(u, color), c_recv.at[u])
+        if KIND[u] == 1:
+            swap_copy(u).start()
         for i in range(3):
-            forward_copy(u, i).start()
-
-    def ring_arrived(u, step, way):
-        sign = 1 - 2 * way
-        if step < 3:
-            at = eighth(got, u, -sign * (step + 1))
+            forward_copy(u, i, False).start()
+
+    def second(u):
+        arrived(part_of(got, u, direct(color, 1 - zp)), s_recv.at[KIND[:u].count(1)])
+        for i in range(3):
+            forward_copy(u, i, True).start()
+
+    def ring_arrived(u, step):
+        arrived(part_of(got, u, 0, 64 if step == 3 else 128), z_recv.at[KIND[:u].count(2), step])
+
+    def circulate(u, step):
+        if step > 0:
+            ring_arrived(u, step - 1)
         else:
-            at = sixteenth(got, u, -sign * (step + 1), way)
-        arrived(at, z_recv.at[u - DIRECT, step, way])
-
-    def circulate(u, step):
+            arrived(mine_of(u, color), c_recv.at[u])
         for way in range(2):
-            if step > 0:
-                ring_arrived(u, step - 1, way)
-            elif way == 0:
-                arrived(eighth(got, u, 0), c_recv.at[u])
             ring_copy(u, step, way).start()
 
     def ready(u):
-        if u < DIRECT:
-            for i, c in enumerate((2, 3, 1)):
-                arrived(piece(got, u, lax.rem(color + c, 4)), f_recv.at[u, i])
+        if KIND[u] == 2:
+            ring_arrived(u, 3)
         else:
-            for way in range(2):
-                ring_arrived(u, 3, way)
+            arrived(part_of(got, u, 0, 384), f_recv.at[u])
 
     def across(units):
         for u in units:
@@ -300,44 +376,30 @@
                 loads[u].wait()
             cross_copy(u).start()
 
-    across(ORDER[:2])
-    own_half(1, v_half)
-
-    def wait_first(j, _):
-        pltpu.make_async_copy(gath.at[j], gath.at[j], g_recv.at[j]).wait()
-        return 0
-
-    lax.fori_loop(0, 16, wait_first, 0)
-    for fr in range(FRAMES):
-        turned = gath[:, fr].astype(F32).reshape(128, 128).T.astype(BF16)
-        blocks[:, fr] = turned.reshape(4, STR, 128)
+    across(ORDER[:EARLY])
 
     def second_copy(e):
         rr, to = quad(e)
-        return remote(blocks.at[rr], held.at[slot], h_send.at[e], h_recv.at[slot], to)
+        return remote(blocks.at[rr], held.at[m, r], sent.at[1], h_recv.at[0], to)
+
+    def relay_copy():
+        return remote(held.at[m], held.at[m], sent.at[2], h_recv.at[1], sibling)
+
+    def relay():
+        arrived(held.at[m], h_recv.at[0])
+        relay_copy().start()
 
     def send_second(e, _):
         second_copy(e).start()
         return 0
 
-    lax.fori_loop(0, 8, send_second, 0)
-
-    across(ORDER[2:])
-    forward(0)
-    forward(1)
-
-    def wait_second(e, _):
-        s = lax.rem(slot + e, 8)
-        pltpu.make_async_copy(held.at[s], held.at[s], h_recv.at[s]).wait()
-        return 0
-
-    lax.fori_loop(0, 8, wait_second, 0)
-    for s in range(8):
-        xp[:, pl.ds(128 * s, 128)] = held[s].reshape(STR * FRAMES, 128)
-    for h in range(2):
-        half = pl.ds(512 * h, 512)
-        placed = dot(xp[...], perm[:, half]).astype(BF16)
-        x[:, half] = dot(rows[...], placed)
+    def turn():
+        arrived(gath, g_recv.at[0])
+        for fr in range(FRAMES):
+            turned = gath[:, fr].astype(F32).reshape(128, 128).T.astype(BF16)
+            blocks[:, fr] = turned.reshape(4, STR, 128)
+        lax.fori_loop(0, 4, send_second, 0)
+        across(ORDER[EARLY:])
 
     def split_norm(values_f32, chunk):
         at = pl.ds(pl.multiple_of(chunk * 32, 32), 32)
@@ -354,14 +416,26 @@
         split_norm(v.reshape(32, 1024), c)
         return 0
 
-    lax.fori_loop(0, 8, first_norm, 0, unroll=4)
-    forward(2)
-    circulate(8, 0)
-
-    load_lk.wait()
-    load_lv.wait()
-
-    def project(u, half, place, center):
+    def norm():
+        arrived(held.at[1 - m], h_recv.at[1])
+        for s in range(8):
+            xp[:, pl.ds(128 * s, 128)] = held[s // 4, s % 4].reshape(STR * FRAMES, 128)
+        for h in range(2):
+            half = pl.ds(512 * h, 512)
+            placed = dot(xp[...], perm[:, half]).astype(BF16)
+            x[:, half] = dot(rows[...], placed)
+        lax.fori_loop(0, 8, first_norm, 0, unroll=4)
+
+    ready_once = set()
+
+    def need(u):
+        if u not in ready_once:
+            ready_once.add(u)
+            ready(u)
+
+    def other_half(u, half, place):
+        need(u)
+
         def memory_rows(c, _):
             at = pl.ds(pl.multiple_of(c * 256, 256), 256)
             sums = half[at, :] + dot(memory[at, theirs], got[u])
@@ -370,28 +444,19 @@
 
         lax.fori_loop(0, 4, memory_rows, 0)
 
-        def group_rows(c, _):
-            at = pl.ds(pl.multiple_of(c * 64, 64), 64)
-            sums = dot(n[f, at, :], own[u]) + dot(n[1 - f, at, :], got[u])
-            g = sums.reshape(8, ROWS, 512)
-            both = jnp.concatenate([g, jnp.zeros_like(g)], axis=1).astype(BF16)
-            place[pl.ds(c * 8, 8), pl.ds(MEM + LEFT, 16), :] = both
-            center[pl.ds(c * 8, 8), :, :] = g[:, :GROUP, :].astype(BF16)
-            return 0
-
-        lax.fori_loop(0, 4, group_rows, 0)
-
-    ready(0)
-    project(0, k_half, keys, center_k)
-    circulate(9, 0)
-    ready(1)
-    project(1, v_half, values, center_v)
-    forward(3)
-    circulate(8, 1)
-    ready(2)
-    q[...] = (
-        (dot(n[f], own[2]) + dot(n[1 - f], got[2])).astype(BF16).astype(F32) * (HD**-0.5)
-    ).reshape(STR, ROWS, 512)
+    def group(u, place, center):
+        need(u)
+
+        g = (dot(n[f], own[u]) + dot(n[1 - f], got[u])).reshape(STR, ROWS, 512)
+        both = jnp.concatenate([g, jnp.zeros_like(g)], axis=1).astype(BF16)
+        place[:, pl.ds(MEM + LEFT, 16), :] = both
+        center[...] = g[:, :GROUP, :].astype(BF16)
+
+    def query():
+        need(2)
+        q[...] = (
+            (dot(n[f], own[2]) + dot(n[1 - f], got[2])).astype(BF16).astype(F32) * (HD**-0.5)
+        ).reshape(STR, ROWS, 512)
 
     heads = ROWS
     head_mask = jnp.where(
@@ -443,31 +508,15 @@
 
         lax.fori_loop(0, 8 // width, few, 0)
 
-    circulate(9, 1)
-    circulate(10, 0)
-    attend_block(0)
-    circulate(8, 2)
-    circulate(11, 0)
-    attend_block(1)
-    circulate(9, 2)
-    attend_block(2)
-    circulate(10, 1)
-    forward(4)
-    attend_block(3)
-
     def exchange(src, dst, i):
         return remote(src, dst, e_send.at[i], e_recv.at[i], sibling)
 
-    ready(3)
-    a = att[...].reshape(STR * ROWS, 512).astype(BF16)
-    part[f] = dot(a, own[3]).astype(BF16)
-    exchange(part.at[f], part_in.at[f], 0).start()
-    part[1 - f] = dot(a, got[3]).astype(BF16)
-    exchange(part.at[1 - f], part_in.at[1 - f], 1).start()
-    circulate(8, 3)
-    circulate(11, 1)
-    exchange(part.at[f], part_in.at[f], 0).wait()
-    exchange(part.at[1 - f], part_in.at[1 - f], 1).wait()
+    def output():
+        need(3)
+        a = att[...].reshape(STR * ROWS, 512).astype(BF16)
+        for i, (h, w) in enumerate(((f, own), (1 - f, got))):
+            part[h] = dot(a, w[3]).astype(BF16)
+            exchange(part.at[h], part_in.at[h], i).start()
 
     def second_norm(c, _):
         at = pl.ds(pl.multiple_of(c * 32, 32), 32)
@@ -477,43 +526,33 @@
         split_norm(normalized(v), c)
         return 0
 
-    lax.fori_loop(0, 8, second_norm, 0, unroll=4)
-    circulate(9, 3)
-    forward(5)
-    mem_next[...] = jnp.tanh(x[...].reshape(STR, ROWS, 1024)[:, FRAMES, :]).astype(BF16)
-
-    def hidden_block(u, pumps):
-        ready(u)
-        sums = dot(n[f], own[u]) + dot(n[1 - f], got[u])
-        hid = jax.nn.gelu(sums, approximate=True).astype(BF16)
-        for pump in pumps:
-            pump()
-        ready(u + 1)
-        return hid
-
-    def pump(u, step=None):
-        return functools.partial(forward, u) if step is None else functools.partial(circulate, u, step)
-
-    hid = hidden_block(8, (pump(10, 2),))
-    down[f] = dot(hid, own[9])
-    down[1 - f] = dot(hid, got[9])
-    circulate(11, 2)
-    forward(6)
-    hid = hidden_block(4, (pump(10, 3),))
-    down[f] += dot(hid, own[5])
-    down[1 - f] += dot(hid, got[5])
-    circulate(11, 3)
-    forward(7)
-    hid = hidden_block(10, ())
-    down[f] += dot(hid, own[11])
-    down[1 - f] += dot(hid, got[11])
-    hid = hidden_block(6, ())
-    down_out[f] = (down[f] + dot(hid, own[7])).astype(BF16)
-    exchange(down_out.at[f], down_in.at[f], 2).start()
-    down_out[1 - f] = (down[1 - f] + dot(hid, got[7])).astype(BF16)
-    exchange(down_out.at[1 - f], down_in.at[1 - f], 3).start()
-    exchange(down_out.at[f], down_in.at[f], 2).wait()
-    exchange(down_out.at[1 - f], down_in.at[1 - f], 3).wait()
+    def norm_two():
+        for i, h in enumerate((f, 1 - f)):
+            exchange(part.at[h], part_in.at[h], i).wait()
+        lax.fori_loop(0, 8, second_norm, 0, unroll=4)
+
+    def next_memory():
+        mem_vm[...] = jnp.tanh(x[...].reshape(STR, ROWS, 1024)[:, FRAMES, :]).astype(BF16)
+        write[1].start()
+
+    hidden = {}
+
+    def hidden_block(j):
+        need(4 + 2 * j)
+        sums = dot(n[f], own[4 + 2 * j]) + dot(n[1 - f], got[4 + 2 * j])
+        hidden[j] = jax.nn.gelu(sums, approximate=True).astype(BF16)
+
+    def down_block(j):
+        need(5 + 2 * j)
+        for i, (h, w) in enumerate(((f, own), (1 - f, got))):
+            sums = dot(hidden[j], w[5 + 2 * j])
+            if j != BLOCKS[0]:
+                sums = down[h] + sums
+            if j != BLOCKS[3]:
+                down[h] = sums
+                continue
+            down_out[h] = sums.astype(BF16)
+            exchange(down_out.at[h], down_in.at[h], 2 + i).start()
 
     def third_norm(c, _):
         at = pl.ds(pl.multiple_of(c * 32, 32), 32)
@@ -522,32 +561,67 @@
         split_norm(normalized(v) * gain[...], c)
         return 0
 
-    lax.fori_loop(0, 8, third_norm, 0, unroll=4)
-    for h in range(2):
-        placed = dot(frames_first[...], n[h]).astype(BF16)
-        out[:, :, pl.ds(512 * h, 512)] = placed.reshape(FRAMES, STR, 512)
-
-    def drain_first(j, _):
-        first_copy(j).wait_send()
-        return 0
-
-    lax.fori_loop(0, 16, drain_first, 0)
-
-    def drain_second(e, _):
-        second_copy(e).wait_send()
-        return 0
-
-    lax.fori_loop(0, 8, drain_second, 0)
-
+    def finish():
+        for i, h in enumerate((f, 1 - f)):
+            exchange(down_out.at[h], down_in.at[h], 2 + i).wait()
+        lax.fori_loop(0, 8, third_norm, 0, unroll=4)
+        for h in range(2):
+            placed = dot(frames_first[...], n[h]).astype(BF16)
+            out_vm[:, :, pl.ds(512 * h, 512)] = placed.reshape(FRAMES, STR, 512)
+        write[0].start()
+
+    def keys_done():
+        load_lk.wait()
+        other_half(0, k_half, keys)
+
+    def values_done():
+        load_lv.wait()
+        other_half(1, v_half, values)
+
+    def group_k():
+        group(0, keys, ck_vm)
+        write[2].start()
+
+    def group_v():
+        group(1, values, cv_vm)
+        write[3].start()
+
+    steps = {
+        "own_v": lambda: own_half(1, v_half),
+        "turn": turn,
+        "norm": norm,
+        "relay": relay,
+        "mem_k": keys_done,
+        "mem_v": values_done,
+        "group_k": group_k,
+        "group_v": group_v,
+        "query": query,
+        "output": output,
+        "norm_two": norm_two,
+        "next": next_memory,
+        "finish": finish,
+    }
+    more = {
+        "forward": forward,
+        "second": second,
+        "circulate": circulate,
+        "attend": attend_block,
+        "hidden": hidden_block,
+        "down": down_block,
+    }
+    for name, *given in STEPS:
+        if name in steps:
+            steps[name]()
+        else:
+            more[name](*given)
+
+    arrived(gath, sent.at[0])
+    arrived(held.at[m], sent.at[1])
+    arrived(held.at[m], sent.at[2])
     for u in range(UNITS):
-        cross_copy(u).wait_send()
-        if u < DIRECT:
-            for i in range(3):
-                forward_copy(u, i).wait_send()
-        else:
-            for step in range(4):
-                for way in range(2):
-                    ring_copy(u, step, way).wait_send()
+        arrived(got.at[u], sent.at[3 + u])
+    for copy in write:
+        copy.wait()
 
 
 def hand_over(*refs):
@@ -598,12 +672,12 @@
         name="layer",
         out_shape=shapes,
         in_specs=[smem] * 2 + [hbm] * 10 + [vmem],
-        out_specs=(vmem,) * 4,
+        out_specs=(hbm,) * 4,
         scratch_shapes=[
             pltpu.VMEM((FRAMES, 8, 4096), BF16),
             pltpu.VMEM((16, FRAMES, 8, 128), BF16),
             pltpu.VMEM((4, FRAMES, STR, 128), BF16),
-            pltpu.VMEM((8, FRAMES, STR, 128), BF16),
+            pltpu.VMEM((2, 4, FRAMES, STR, 128), BF16),
             pltpu.VMEM((1024, 1024), BF16),
             pltpu.VMEM((STR * ROWS, STR * FRAMES), BF16),
             pltpu.VMEM((STR * FRAMES, STR * ROWS), BF16),
@@ -624,17 +698,16 @@
             pltpu.VMEM((2, STR * ROWS, 512), BF16),
             pltpu.VMEM((STR * MEM, 512), F32),
             pltpu.VMEM((STR * MEM, 512), F32),
+            *[pltpu.VMEM(v.shape, v.dtype) for v in shapes],
+            dma((4,)),
             dma((UNITS + 4,)),
-            dma((16,)),
-            dma((16,)),
-            dma((8,)),
-            dma((8,)),
+            dma((3 + UNITS,)),
+            dma((1,)),
+            dma((2,)),
             dma((UNITS,)),
+            dma((max(1, KIND.count(1)),)),
             dma((UNITS,)),
-            dma((DIRECT, 3)),
-            dma((DIRECT, 3)),
-            dma((UNITS - DIRECT, 4, 2)),
-            dma((UNITS - DIRECT, 4, 2)),
+            dma((max(1, KIND.count(2)), 4)),
             dma((4,)),
             dma((4,)),
         ],

time: 68.1 us -> 55.5 us (0.81)
  Pallas kernels: 67.4 us -> 54.8 us
    pallas_call x1, Pallas kernels: 65.5 us -> 52.9 us  [shards(): pl.pallas_call(kernel, name='layer', out_shape=shapes, in_specs=[smem] *...]
where the time goes in v3:
time: 55.5 us; the launch traced here: 55.4 us
  Pallas kernels  54.8 us (99%)
  between operations  0.64 us (1%)
    pallas_call x1, Pallas kernels, shards(): pl.pallas_call(kernel, name='layer', out_shape=shapes, in_specs=[smem] *...  52.9 us
    pallas_call x1, Pallas kernels, shards(): pl.pallas_call(hand_over, name='hand_over', out_shape=shapes, in_specs=[h...  1.87 us

profile of v3, /device:TPU:1, one launch (start us, length us, event | category | flops | bytes accessed | tf_op | source)
XLA Modules:
  0.0 55.4 jit_solution(4120025106008760666)
XLA Ops:
  0.6 52.9 %layer.1 = (bf16[5,32,1024]{2,1,0:T(8,128)(2,1)}, bf16[32,1024]{1,0:T(8,128)(2,1)}, bf16[32,4,512]{2,1,0:T(4,128)(2,1)}, bf16[32,4,512]{2,1,0:T(4,128)(2,1)}) custom-call(s32[32]{0:T(128)} %fill.1, s32[32]{0:T(128)} %length.1, bf16[5,8,4096]{2,1,0:T(8,128)(2,1)} %feat_hbm.1, bf16[1024,1024]{1,0:T(8,128)(2,1)} %bitcast.3, bf16[32,64,512]{2,1,0:T(8,128)(2,1)} %lk_hbm.1, ...), custom_call_target="tpu_custom_call" | custom-call | tf_op jit(solution)/shard_map/layer/pallas_call | solution.py:670
  53.5 1.9 %hand_over.1 = (bf16[5,32,1024]{2,1,0:T(8,128)(2,1)}, bf16[32,1024]{1,0:T(8,128)(2,1)}, bf16[32,4,512]{2,1,0:T(4,128)(2,1)}, bf16[32,4,512]{2,1,0:T(4,128)(2,1)}) custom-call(bf16[5,32,1024]{2,1,0:T(8,128)(2,1)} %get-tuple-element.12.refs_0_, bf16[32,1024]{1,0:T(8,128)(2,1)} %get-tuple-element.13.refs_1_, bf16[32,4,512]{2,1,0:T(4,128)(2,1)} %get-tuple-element.14.refs_2_, ...), custom_call_target="tpu_custom_call" | custom-call | tf_op jit(solution)/shard_map/hand_over/pallas_call | solution.py:732

commit v4 on v3

--- a/solution.py
+++ b/solution.py
@@ -16,61 +16,60 @@
 ROWS = 8
 KEYS = 112
 UNITS = 12
-KIND = (1, 1, 1, 1, 2, 2, 1, 0, 2, 0, 0, 0)
-ORDER = (1, 0, 2, 6, 3, 4, 5, 8, 7, 10, 11, 9)
+KIND = (1, 1, 1, 0, 2, 0, 2, 0, 0, 1, 2, 0)
+ORDER = (1, 2, 0, 4, 10, 6, 9, 3, 11, 5, 8, 7)
 EARLY = 4
-BLOCKS = (3, 1, 0, 2)
+BLOCKS = (0, 2, 3, 1)
 STEPS = (
     ("own_v", 0),
     ("forward", 1),
     ("turn", 0),
+    ("forward", 2),
     ("forward", 0),
-    ("forward", 2),
     ("second", 1),
-    ("forward", 6),
+    ("circulate", 4, 0),
     ("relay", 0),
+    ("second", 2),
+    ("circulate", 10, 0),
+    ("norm", 0),
     ("second", 0),
+    ("circulate", 6, 0),
+    ("mem_v", 0),
+    ("forward", 9),
+    ("circulate", 4, 1),
+    ("group_v", 0),
+    ("query", 0),
+    ("circulate", 10, 1),
     ("forward", 3),
-    ("norm", 0),
-    ("second", 2),
-    ("circulate", 4, 0),
-    ("second", 6),
-    ("mem_v", 0),
-    ("circulate", 5, 0),
-    ("group_v", 0),
-    ("second", 3),
-    ("circulate", 8, 0),
     ("mem_k", 0),
-    ("circulate", 4, 1),
     ("group_k", 0),
-    ("forward", 7),
-    ("circulate", 5, 1),
-    ("query", 0),
+    ("circulate", 6, 1),
+    ("second", 9),
     ("attend", 0),
-    ("circulate", 8, 1),
+    ("forward", 11),
     ("attend", 1),
-    ("forward", 10),
     ("circulate", 4, 2),
     ("attend", 2),
-    ("circulate", 5, 2),
+    ("forward", 5),
+    ("circulate", 10, 2),
     ("attend", 3),
-    ("forward", 11),
     ("output", 0),
-    ("circulate", 8, 2),
+    ("circulate", 6, 2),
+    ("forward", 8),
+    ("norm_two", 0),
+    ("next", 0),
     ("circulate", 4, 3),
-    ("norm_two", 0),
-    ("forward", 9),
-    ("next", 0),
-    ("circulate", 5, 3),
-    ("hidden", 3),
-    ("circulate", 8, 3),
-    ("down", 3),
-    ("hidden", 1),
-    ("down", 1),
+    ("circulate", 10, 3),
+    ("forward", 7),
+    ("circulate", 6, 3),
     ("hidden", 0),
     ("down", 0),
     ("hidden", 2),
     ("down", 2),
+    ("hidden", 3),
+    ("down", 3),
+    ("hidden", 1),
+    ("down", 1),
     ("finish", 0),
 )
 EPS = 1e-05
@@ -91,8 +90,8 @@
 
 
 def kernel(
-    fill,
-    length,
+    fill_hbm,
+    length_hbm,
     feat_hbm,
     mem_hbm,
     lk_hbm,
@@ -103,7 +102,7 @@
     wo_hbm,
     wu_hbm,
     wd_hbm,
-    gain,
+    gain_hbm,
     out,
     mem_next,
     center_k,
@@ -136,6 +135,9 @@
     mem_vm,
     ck_vm,
     cv_vm,
+    fill,
+    length,
+    gain,
     o_sem,
     l_sem,
     sent,
@@ -202,6 +204,42 @@
     load_mem = load(UNITS + 1, mem_hbm, memory)
     load_lk = load(UNITS + 2, lk_hbm, keys.at[:, pl.ds(MEM, LEFT), :])
     load_lv = load(UNITS + 3, lv_hbm, values.at[:, pl.ds(MEM, LEFT), :])
+    small = [
+        load(UNITS + 4, fill_hbm, fill),
+        load(UNITS + 5, length_hbm, length),
+        load(UNITS + 6, gain_hbm, gain),
+    ]
+    barrier = pltpu.get_barrier_semaphore()
+
+    def greet(to):
+        pl.semaphore_signal(
+            barrier, inc=1, device_id=to, device_id_type=pl.DeviceIdType.MESH
+        )
+
+    def greet_sources(j, _):
+        kk = 2 * j + m
+        greet(dev(2 * kk + odd, f, 1 - lax.rem(k, 2)))
+        return 0
+
+    lax.fori_loop(0, 16, greet_sources, 0)
+
+    def quad(e):
+        rr = lax.rem(r + e, 4)
+        return rr, dev(2 * over + lax.div(rr, 2), lax.rem(rr, 2), m)
+
+    def greet_quad(e, _):
+        greet(quad(e)[1])
+        return 0
+
+    lax.fori_loop(0, 4, greet_quad, 0)
+    greet(cross_dev)
+    for to in ring:
+        greet(to)
+    greet(sibling)
+    greet(z_up)
+    greet(z_down)
+    greet(z_pair)
+
     load_feat.start()
     loads[0].start()
     load_mem.start()
@@ -210,37 +248,8 @@
             loads[u].start()
     load_lk.start()
     load_lv.start()
-
-    barrier = pltpu.get_barrier_semaphore()
-
-    def greet(to):
-        pl.semaphore_signal(
-            barrier, inc=1, device_id=to, device_id_type=pl.DeviceIdType.MESH
-        )
-
-    def greet_sources(j, _):
-        kk = 2 * j + m
-        greet(dev(2 * kk + odd, f, 1 - lax.rem(k, 2)))
-        return 0
-
-    lax.fori_loop(0, 16, greet_sources, 0)
-
-    def quad(e):
-        rr = lax.rem(r + e, 4)
-        return rr, dev(2 * over + lax.div(rr, 2), lax.rem(rr, 2), m)
-
-    def greet_quad(e, _):
-        greet(quad(e)[1])
-        return 0
-
-    lax.fori_loop(0, 4, greet_quad, 0)
-    greet(cross_dev)
-    for to in ring:
-        greet(to)
-    greet(sibling)
-    greet(z_up)
-    greet(z_down)
-    greet(z_pair)
+    for c in small:
+        c.start()
 
     def build_perm(s, _):
         at = lax.broadcasted_iota(jnp.int32, (128, 1024), 0)
@@ -467,7 +476,7 @@
     )
     queries = FRAMES + 1
 
-    width = 4
+    width = 8
 
     def attend(first):
         streams = [first + i for i in range(width)]
@@ -571,6 +580,8 @@
         write[0].start()
 
     def keys_done():
+        for c in small:
+            c.wait()
         load_lk.wait()
         other_half(0, k_half, keys)
 
@@ -625,18 +636,10 @@
 
 
 def hand_over(*refs):
-    given, held, results, into, out_of = refs[:4], refs[4:8], refs[8:12], refs[12], refs[13]
-    arrive = [
-        pltpu.make_async_copy(*pair, into.at[i]) for i, pair in enumerate(zip(given, results))
-    ]
-    leave = [
-        pltpu.make_async_copy(*pair, out_of.at[i]) for i, pair in enumerate(zip(results, held))
-    ]
-    for copy in arrive:
+    sems = refs[8]
+    leave = [pltpu.make_async_copy(refs[i], refs[4 + i], sems.at[i]) for i in range(4)]
+    for copy in leave:
         copy.start()
-    for i in range(4):
-        arrive[i].wait()
-        leave[i].start()
     for copy in leave:
         copy.wait()
 
@@ -657,9 +660,8 @@
     out_gain,
 ):
     memory = memory_bank.reshape(STR * MEM, 1024)
-    smem = pl.BlockSpec(memory_space=pltpu.SMEM)
     hbm = pl.BlockSpec(memory_space=pltpu.HBM)
-    vmem = pl.BlockSpec(memory_space=pltpu.VMEM)
+    either = pl.BlockSpec(memory_space=pl.ANY)
     dma = pltpu.SemaphoreType.DMA
     shapes = (
         jax.ShapeDtypeStruct((FRAMES, STR, 1024), BF16),
@@ -671,8 +673,8 @@
         kernel,
         name="layer",
         out_shape=shapes,
-        in_specs=[smem] * 2 + [hbm] * 10 + [vmem],
-        out_specs=(hbm,) * 4,
+        in_specs=[hbm] * 13,
+        out_specs=(either,) * 4,
         scratch_shapes=[
             pltpu.VMEM((FRAMES, 8, 4096), BF16),
             pltpu.VMEM((16, FRAMES, 8, 128), BF16),
@@ -699,8 +701,11 @@
             pltpu.VMEM((STR * MEM, 512), F32),
             pltpu.VMEM((STR * MEM, 512), F32),
             *[pltpu.VMEM(v.shape, v.dtype) for v in shapes],
+            pltpu.SMEM((STR,), jnp.int32),
+            pltpu.SMEM((STR,), jnp.int32),
+            pltpu.VMEM((1, 1024), F32),
             dma((4,)),
-            dma((UNITS + 4,)),
+            dma((UNITS + 7,)),
             dma((3 + UNITS,)),
             dma((1,)),
             dma((2,)),
@@ -712,31 +717,36 @@
             dma((4,)),
         ],
         compiler_params=pltpu.CompilerParams(
-            collective_id=0, has_side_effects=True, vmem_limit_bytes=62_600_000
+            collective_id=0, has_side_effects=True, vmem_limit_bytes=46_000_000
         ),
     )(
-        memory_fill,
-        left_length,
-        features,
-        memory,
-        left_keys,
-        left_values,
-        w_query,
-        w_key,
-        w_value,
-        w_out,
-        w_up,
-        w_down,
-        out_gain.reshape(1, 1024),
+        *[
+            pltpu.with_memory_space_constraint(v, pltpu.HBM)
+            for v in (
+                memory_fill,
+                left_length,
+                features,
+                memory,
+                left_keys,
+                left_values,
+                w_query,
+                w_key,
+                w_value,
+                w_out,
+                w_up,
+                w_down,
+                out_gain.reshape(1, 1024),
+            )
+        ]
     )
     layer_out, memory_next, center_keys, center_values = pl.pallas_call(
         hand_over,
         name="hand_over",
         out_shape=shapes,
-        in_specs=[hbm] * 4,
+        in_specs=[either] * 4,
         out_specs=(hbm,) * 4,
-        scratch_shapes=[pltpu.VMEM(v.shape, v.dtype) for v in shapes] + [dma((4,)), dma((4,))],
-        compiler_params=pltpu.CompilerParams(vmem_limit_bytes=62_600_000),
+        scratch_shapes=[dma((4,))],
+        compiler_params=pltpu.CompilerParams(vmem_limit_bytes=1_000_000),
     )(*results)
     return jnp.transpose(layer_out, (1, 0, 2)), memory_next, center_keys, center_values
 

time: 55.5 us -> 53.4 us (0.962)
  Pallas kernels: 54.8 us -> 52.7 us
    pallas_call x2, Pallas kernels: 54.8 us -> 52.7 us  [the longest x1 51.8 us: shards(): pl.pallas_call(kernel, name='layer', out_shape=shapes, in_specs=[hbm] * 1...]
where the time goes in v4:
time: 53.4 us; the launch traced here: 53.3 us
  Pallas kernels  52.7 us (99%)
  between operations  0.64 us (1%)
    pallas_call x1, Pallas kernels, shards(): pl.pallas_call(kernel, name='layer', out_shape=shapes, in_specs=[hbm] * 1...  51.8 us

profile of v4, /device:TPU:1, one launch (start us, length us, event | category | flops | bytes accessed | tf_op | source)
XLA Modules:
  0.0 53.3 jit_solution(13867837972856837665)
XLA Ops:
  0.6 51.8 %layer.1 = (bf16[5,32,1024]{2,1,0:T(8,128)(2,1)S(1)}, bf16[32,1024]{1,0:T(8,128)(2,1)S(1)}, bf16[32,4,512]{2,1,0:T(4,128)(2,1)S(1)}, bf16[32,4,512]{2,1,0:T(4,128)(2,1)S(1)}) custom-call(s32[32]{0:T(128)} %fill_hbm.1, s32[32]{0:T(128)} %length_hbm.1, bf16[5,8,4096]{2,1,0:T(8,128)(2,1)} %feat_hbm.1, bf16[1024,1024]{1,0:T(8,128)(2,1)} %bitcast.3, ...), custom_call_target="tpu_custom_call" | custom-call | tf_op jit(solution)/shard_map/layer/pallas_call | solution.py:672
  52.5 0.9 %hand_over.1 = (bf16[5,32,1024]{2,1,0:T(8,128)(2,1)}, bf16[32,1024]{1,0:T(8,128)(2,1)}, bf16[32,4,512]{2,1,0:T(4,128)(2,1)}, bf16[32,4,512]{2,1,0:T(4,128)(2,1)}) custom-call(bf16[5,32,1024]{2,1,0:T(8,128)(2,1)S(1)} %get-tuple-element.12.refs_0_, bf16[32,1024]{1,0:T(8,128)(2,1)S(1)} %get-tuple-element.13.refs_1_, ...), custom_call_target="tpu_custom_call" | custom-call | tf_op jit(solution)/shard_map/hand_over/pallas_call | solution.py:742

commit v5 on v4

--- a/solution.py
+++ b/solution.py
@@ -59,8 +59,8 @@
     ("norm_two", 0),
     ("next", 0),
     ("circulate", 4, 3),
+    ("forward", 7),
     ("circulate", 10, 3),
-    ("forward", 7),
     ("circulate", 6, 3),
     ("hidden", 0),
     ("down", 0),
@@ -251,24 +251,6 @@
     for c in small:
         c.start()
 
-    def build_perm(s, _):
-        at = lax.broadcasted_iota(jnp.int32, (128, 1024), 0)
-        col = lax.broadcasted_iota(jnp.int32, (128, 1024), 1)
-        want = (at >> 3) * 64 + lax.div(s, 4) * 32 + lax.rem(s, 4) * 8 + (at & 7)
-        perm[pl.ds(pl.multiple_of(s * 128, 128), 128), :] = jnp.where(
-            col == want, 1.0, 0.0
-        ).astype(BF16)
-        return 0
-
-    lax.fori_loop(0, 8, build_perm, 0)
-    at = lax.broadcasted_iota(jnp.int32, (STR * ROWS, STR * FRAMES), 0)
-    col = lax.broadcasted_iota(jnp.int32, (STR * ROWS, STR * FRAMES), 1)
-    rows[...] = jnp.where(col == (at & 7) * STR + (at >> 3), 1.0, 0.0).astype(BF16)
-    at = lax.broadcasted_iota(jnp.int32, (STR * FRAMES, STR * ROWS), 0)
-    col = lax.broadcasted_iota(jnp.int32, (STR * FRAMES, STR * ROWS), 1)
-    frames_first[...] = jnp.where(col == (at & 31) * ROWS + (at >> 5), 1.0, 0.0).astype(BF16)
-    att[...] = jnp.zeros_like(att)
-
     mine = pl.ds(pl.multiple_of(f * 512, 512), 512)
     theirs = pl.ds(pl.multiple_of((1 - f) * 512, 512), 512)
 
@@ -280,9 +262,6 @@
 
         lax.fori_loop(0, 4, memory_rows, 0)
 
-    loads[0].wait()
-    load_mem.wait()
-    own_half(0, k_half)
     pl.semaphore_wait(barrier, 16 + 4 + 1 + 3 + 1 + 2 + 1)
 
     def first_copy(j):
@@ -381,11 +360,34 @@
 
     def across(units):
         for u in units:
-            if u > 0:
+            if u > 0 or u in ORDER[:EARLY]:
                 loads[u].wait()
             cross_copy(u).start()
 
     across(ORDER[:EARLY])
+
+    def build_perm(s, _):
+        at = lax.broadcasted_iota(jnp.int32, (128, 1024), 0)
+        col = lax.broadcasted_iota(jnp.int32, (128, 1024), 1)
+        want = (at >> 3) * 64 + lax.div(s, 4) * 32 + lax.rem(s, 4) * 8 + (at & 7)
+        perm[pl.ds(pl.multiple_of(s * 128, 128), 128), :] = jnp.where(
+            col == want, 1.0, 0.0
+        ).astype(BF16)
+        return 0
+
+    lax.fori_loop(0, 8, build_perm, 0)
+    at = lax.broadcasted_iota(jnp.int32, (STR * ROWS, STR * FRAMES), 0)
+    col = lax.broadcasted_iota(jnp.int32, (STR * ROWS, STR * FRAMES), 1)
+    rows[...] = jnp.where(col == (at & 7) * STR + (at >> 3), 1.0, 0.0).astype(BF16)
+    at = lax.broadcasted_iota(jnp.int32, (STR * FRAMES, STR * ROWS), 0)
+    col = lax.broadcasted_iota(jnp.int32, (STR * FRAMES, STR * ROWS), 1)
+    frames_first[...] = jnp.where(col == (at & 31) * ROWS + (at >> 5), 1.0, 0.0).astype(BF16)
+    att[...] = jnp.zeros_like(att)
+
+    load_mem.wait()
+    if 0 not in ORDER[:EARLY]:
+        loads[0].wait()
+    own_half(0, k_half)
 
     def second_copy(e):
         rr, to = quad(e)

time: 53.4 us -> 53.3 us (level)
  no operation moved by 1% of the time
where the time goes in v5:
time: 53.3 us
  Pallas kernels  52.6 us (99%)
  between operations  0.64 us (1%)
    pallas_call x1, Pallas kernels, shards(): pl.pallas_call(kernel, name='layer', out_shape=shapes, in_specs=[hbm] * 1...  51.7 us

profile of v5, /device:TPU:1, one launch (start us, length us, event | category | flops | bytes accessed | tf_op | source)
XLA Modules:
  0.0 53.3 jit_solution(12671991004356667619)
XLA Ops:
  0.6 51.7 %layer.1 = (bf16[5,32,1024]{2,1,0:T(8,128)(2,1)S(1)}, bf16[32,1024]{1,0:T(8,128)(2,1)S(1)}, bf16[32,4,512]{2,1,0:T(4,128)(2,1)S(1)}, bf16[32,4,512]{2,1,0:T(4,128)(2,1)S(1)}) custom-call(s32[32]{0:T(128)} %fill_hbm.1, s32[32]{0:T(128)} %length_hbm.1, bf16[5,8,4096]{2,1,0:T(8,128)(2,1)} %feat_hbm.1, bf16[1024,1024]{1,0:T(8,128)(2,1)} %bitcast.3, ...), custom_call_target="tpu_custom_call" | custom-call | tf_op jit(solution)/shard_map/layer/pallas_call | solution.py:674
  52.4 0.9 %hand_over.1 = (bf16[5,32,1024]{2,1,0:T(8,128)(2,1)}, bf16[32,1024]{1,0:T(8,128)(2,1)}, bf16[32,4,512]{2,1,0:T(4,128)(2,1)}, bf16[32,4,512]{2,1,0:T(4,128)(2,1)}) custom-call(bf16[5,32,1024]{2,1,0:T(8,128)(2,1)S(1)} %get-tuple-element.12.refs_0_, bf16[32,1024]{1,0:T(8,128)(2,1)S(1)} %get-tuple-element.13.refs_1_, ...), custom_call_target="tpu_custom_call" | custom-call | tf_op jit(solution)/shard_map/hand_over/pallas_call | solution.py:744
